TPU v7x, 32 devices: a whole 2x2x4 slice. The times are simulated.
32 devices in a mesh: batch: 2 (over x), w: 4 (over z), h: 4 (over y, core).
Axes of the slice: x: 2, y: 2, z: 4, core: 2. Of those that a mesh axis runs over, the one named last changes fastest.
Arguments:
- image: bfloat16 [384, 1024, 32, 1], P('batch', 'h', 'w'), parts along dimension 0
- down_w1: bfloat16 [3, 3, 1, 64], replicated
- down_v1: float32 [3, 64], replicated
- refine_w1: bfloat16 [3, 3, 64, 64], replicated
- refine_v1: float32 [3, 64], replicated
- down_w2: bfloat16 [3, 3, 64, 128], replicated
- down_v2: float32 [3, 128], replicated
- refine_w2: bfloat16 [3, 3, 128, 128], replicated
- refine_v2: float32 [3, 128], replicated
- down_w3: bfloat16 [3, 3, 128, 256], replicated
- down_v3: float32 [3, 256], replicated
- refine_w3: bfloat16 [3, 3, 256, 256], replicated
- refine_v3: float32 [3, 256], replicated
Outputs:
- output: bfloat16 [384, 128, 4, 256], P('batch', 'h', 'w'), parts along dimension 0
There are 2 independent parts. A program takes and returns all parts, laid end to end along the dimension named above; an argument that names none is the same for every part.
All inputs are finite; a program needn't handle non-finite values.
Results may differ from a plain program's by a relative error of at most 0.00397023.
Values are sent between devices in bfloat16 or wider.
A program may use at most 1 GiB of HBM per device.

v0:
```python
import jax
import jax.numpy as jnp
from jax import lax
from jax.sharding import PartitionSpec as P

NORM_GROUPS = 8
NORM_EPS = 1e-5


def shift_in(piece, axis_name, axis_size, from_lower):
    if axis_size == 1:
        return jnp.zeros_like(piece)
    if from_lower:
        send_pairs = [(source, source + 1) for source in range(axis_size - 1)]
    else:
        send_pairs = [(source + 1, source) for source in range(axis_size - 1)]
    return lax.ppermute(piece, axis_name, send_pairs)


def lower_halo(tile, row_count, col_count):
    above = shift_in(tile[:, -1:], "h", row_count, True)
    tall = jnp.concatenate([above, tile], axis=1)
    left = shift_in(tall[:, :, -1:], "w", col_count, True)
    return jnp.concatenate([left, tall], axis=2)


def both_halo(tile, row_count, col_count):
    above = shift_in(tile[:, -1:], "h", row_count, True)
    below = shift_in(tile[:, :1], "h", row_count, False)
    tall = jnp.concatenate([above, tile, below], axis=1)
    left = shift_in(tall[:, :, -1:], "w", col_count, True)
    right = shift_in(tall[:, :, :1], "w", col_count, False)
    return jnp.concatenate([left, tall, right], axis=2)


def norm_apply(summed, affine, totals, pixel_count, per_group):
    grp_mean = totals[0] / pixel_count
    grp_var = jnp.maximum(totals[1] / pixel_count - jnp.square(grp_mean), 0.0)
    inv_std = lax.rsqrt(grp_var + NORM_EPS)
    chan_scale = jnp.repeat(inv_std, per_group, axis=1) * affine[1]
    chan_shift = affine[2] - jnp.repeat(grp_mean * inv_std, per_group, axis=1) * affine[1]
    return jax.nn.relu(summed * chan_scale[:, None, None, :] + chan_shift[:, None, None, :]).astype(jnp.bfloat16)


def conv_norm(padded, kernel, affine, stride, spatial_devices):
    summed = lax.conv_general_dilated(padded, kernel, (stride, stride), "VALID", dimension_numbers=("NHWC", "HWIO", "NHWC"), preferred_element_type=jnp.float32) + affine[0]
    out_shape = summed.shape
    per_group = out_shape[3] // NORM_GROUPS
    pixel_count = out_shape[1] * out_shape[2] * spatial_devices * per_group
    part_sums = jnp.stack([jnp.sum(summed, axis=(1, 2)), jnp.sum(jnp.square(summed), axis=(1, 2))])
    part_sums = jnp.sum(part_sums.reshape(2, out_shape[0], NORM_GROUPS, per_group), axis=3)
    totals = lax.psum(part_sums, ("h", "w"))
    return norm_apply(summed, affine, totals, pixel_count, per_group)


def solution(mesh):
    row_count = mesh.shape["h"]
    col_count = mesh.shape["w"]
    spatial_devices = row_count * col_count
    act_spec = P("batch", "h", "w")

    def local_forward(tile, *params):
        current = tile
        for stage in range(3):
            down_w, down_v, refine_w, refine_v = params[4 * stage:4 * stage + 4]
            current = conv_norm(lower_halo(current, row_count, col_count), down_w, down_v, 2, spatial_devices)
            current = conv_norm(both_halo(current, row_count, col_count), refine_w, refine_v, 1, spatial_devices)
        return current

    return jax.shard_map(local_forward, mesh=mesh, in_specs=(act_spec,) + (P(),) * 12, out_specs=act_spec, check_vma=False)
```

profile of v0, /device:TPU:0, one launch (start us, length us, event | category | flops | bytes accessed | tf_op | source)
XLA Modules:
  0.0 997.5 jit_solution(2097975008346675768)
XLA Ops:
  0.0 4.6 copy.38
  8.3 4.3 collective-permute-start.1
  13.4 5.1 collective-permute-done.1
  18.5 18.4 %add_reduce_fusion.1 = (f32[192,64]{0,1:T(8,128)S(1)}, f32[192,64]{0,1:T(8,128)S(1)}, f32[192,128,4,64]{0,3,2,1:T(8,128)}) fusion(f32[64]{0:T(128)S(1)} %get-tuple-element.55, bf16[3,3,1,64]{3,1,2,0:T(4,128)(2,1)} %param.14, bf16[192,256,8,1]{0,3,2,1:T(2,128)(2,1)S(1)} %copy.38, bf16[192,1,8,1]{0,3,2,1:T(2,128)(2,1)S(1)} %collective-permute-done, ...), kind=kOutput, calls=%fused_computation.5 | convolution fusion | flops 141052032 | bytes 26153728 | tf_op jit(solution)/shard_map/conv_general_dilated | solution.py:46
  36.9 60.3 %psum.42 = f32[2,192,8]{1,2,0:T(8,128)S(1)} all-reduce(f32[2,192,8]{1,2,0:T(8,128)S(1)} %maximum_reduce_fusion.4), channel_id=1, replica_groups=mesh['batch'=2,'w'=4,'h'=4] {'h','w'}, use_global_device_ids=true, to_apply=%region_3.0 | all-reduce | flops 3072 | bytes 24576 | tf_op jit(solution)/shard_map/psum | solution.py:52
  97.3 13.8 %maximum_convert_fusion.1 = bf16[192,128,4,64]{0,3,2,1:T(8,128)(2,1)S(1)} fusion(f32[192,128,4,64]{0,3,2,1:T(8,128)} %get-tuple-element.69, f32[192,64]{0,1:T(8,128)S(1)} %get-tuple-element.68, f32[192,64]{0,1:T(8,128)S(1)} %get-tuple-element.67, f32[64]{0:T(128)S(1)} %get-tuple-element.55), kind=kLoop, calls=%fused_computation.2 | loop fusion | flops 31457280 | bytes 37847296 | tf_op jit(solution)/shard_map/convert_element_type | solution.py:42
  114.0 5.9 collective-permute-done.3
  125.7 87.9 %collective-permute-done.4 = bf16[192,130,1,64]{0,3,2,1:T(8,128)(2,1)S(1)} collective-permute-done((bf16[192,130,1,64]{0,3,2,1:T(8,128)(2,1)S(1)}, bf16[192,130,1,64]{0,3,2,1:T(8,128)(2,1)S(1)}, u32[]{:S(2)}, u32[]{:S(2)}) %collective-permute-start.4) | collective-permute-done | bytes 3194912 | tf_op jit(solution)/shard_map/ppermute | solution.py:17
  213.6 5.0 collective-permute-done.5
  220.7 36.7 %add_reduce_fusion = (f32[192,64]{0,1:T(8,128)S(1)}, f32[192,64]{0,1:T(8,128)S(1)}, f32[192,128,4,64]{0,3,2,1:T(8,128)}) fusion(f32[64]{0:T(128)S(1)} %get-tuple-element.52, bf16[3,3,64,64]{3,2,1,0:T(8,128)(2,1)S(1)} %copy-done.11, bf16[192,130,1,64]{0,3,2,1:T(8,128)(2,1)} %copy-done.7, bf16[192,1,4,64]{0,3,2,1:T(8,128)(2,1)S(1)} %collective-permute-done.3, ...), kind=kOutput, calls=%fused_computation.4 | convolution fusion | flops 7311237120 | bytes 44507392 | tf_op jit(solution)/shard_map/conv_general_dilated | solution.py:46
  257.4 58.8 %psum.43 = f32[2,192,8]{1,2,0:T(8,128)S(1)} all-reduce(f32[2,192,8]{1,2,0:T(8,128)S(1)} %maximum_reduce_fusion.5), channel_id=1, replica_groups=mesh['batch'=2,'w'=4,'h'=4] {'h','w'}, use_global_device_ids=true, to_apply=%region_7.8 | all-reduce | flops 3072 | bytes 24576 | tf_op jit(solution)/shard_map/psum | solution.py:52
  316.3 13.8 %maximum_convert_fusion = bf16[192,128,4,64]{0,3,2,1:T(8,128)(2,1)S(1)} fusion(f32[192,128,4,64]{0,3,2,1:T(8,128)} %get-tuple-element.70, f32[192,64]{0,1:T(8,128)S(1)} %get-tuple-element.66, f32[192,64]{0,1:T(8,128)S(1)} %get-tuple-element.65, f32[64]{0:T(128)S(1)} %get-tuple-element.52), kind=kLoop, calls=%fused_computation | loop fusion | flops 31457280 | bytes 37847296 | tf_op jit(solution)/shard_map/convert_element_type | solution.py:42
  335.1 88.3 %collective-permute-done.7 = bf16[192,129,1,64]{0,3,2,1:T(8,128)(2,1)S(1)} collective-permute-done((bf16[192,129,1,64]{0,3,2,1:T(8,128)(2,1)S(1)}, bf16[192,129,1,64]{0,3,2,1:T(8,128)(2,1)S(1)}, u32[]{:S(2)}, u32[]{:S(2)}) %collective-permute-start.7) | collective-permute-done | bytes 3170336 | tf_op jit(solution)/shard_map/ppermute | solution.py:17
  425.4 15.1 %add_reduce_fusion.3 = (f32[192,128]{1,0:T(8,128)S(1)}, f32[192,128]{1,0:T(8,128)S(1)}, f32[192,64,2,128]{3,0,2,1:T(8,128)}) fusion(f32[128]{0:T(128)S(1)} %get-tuple-element.49, bf16[3,3,64,128]{3,2,1,0:T(8,128)(2,1)S(1)} %copy-done.12, bf16[192,128,4,64]{0,3,2,1:T(8,128)(2,1)S(1)} %maximum_convert_fusion, ...), kind=kOutput, calls=%fused_computation.37 | convolution fusion | flops 3652263936 | bytes 28779008 | tf_op jit(solution)/shard_map/conv_general_dilated | solution.py:46
  440.8 60.9 %psum.44 = f32[2,192,8]{1,2,0:T(8,128)S(1)} all-reduce(f32[2,192,8]{1,2,0:T(8,128)S(1)} %maximum_reduce_fusion.2), channel_id=1, replica_groups=mesh['batch'=2,'w'=4,'h'=4] {'h','w'}, use_global_device_ids=true, to_apply=%region_11.12 | all-reduce | flops 3072 | bytes 24576 | tf_op jit(solution)/shard_map/psum | solution.py:52
  502.0 9.7 maximum_convert_fusion.3
  515.2 7.0 collective-permute-done.9
  522.2 4.2 pad_maximum_fusion
  531.1 66.3 %collective-permute-done.10 = bf16[192,66,1,128]{3,0,2,1:T(8,128)(2,1)S(1)} collective-permute-done((bf16[192,66,1,128]{3,0,2,1:T(8,128)(2,1)S(1)}, bf16[192,66,1,128]{3,0,2,1:T(8,128)(2,1)S(1)}, u32[]{:S(2)}, u32[]{:S(2)}) %collective-permute-start.10) | collective-permute-done | bytes 3244064 | tf_op jit(solution)/shard_map/ppermute | solution.py:17
  597.3 4.9 collective-permute-done.11
  602.3 17.3 %add_reduce_fusion.2 = (f32[192,128]{1,0:T(8,128)S(1)}, f32[192,128]{1,0:T(8,128)S(1)}, f32[192,64,2,128]{3,0,2,1:T(8,128)}) fusion(f32[128]{0:T(128)S(1)} %get-tuple-element.46, bf16[3,3,128,128]{3,2,1,0:T(8,128)(2,1)S(1)} %copy-done.10, bf16[192,66,1,128]{3,0,2,1:T(8,128)(2,1)S(1)} %collective-permute-done.11, ...), kind=kOutput, calls=%fused_computation.36 | convolution fusion | flops 7286243328 | bytes 26051072 | tf_op jit(solution)/shard_map/conv_general_dilated | solution.py:46
  619.8 58.7 %psum.45 = f32[2,192,8]{1,2,0:T(8,128)S(1)} all-reduce(f32[2,192,8]{1,2,0:T(8,128)S(1)} %maximum_reduce_fusion.3), channel_id=1, replica_groups=mesh['batch'=2,'w'=4,'h'=4] {'h','w'}, use_global_device_ids=true, to_apply=%region_15.16 | all-reduce | flops 3072 | bytes 24576 | tf_op jit(solution)/shard_map/psum | solution.py:52
  678.8 9.7 maximum_convert_fusion.2
  695.8 67.0 %collective-permute-done.13 = bf16[192,65,1,128]{3,0,2,1:T(8,128)(2,1)S(1)} collective-permute-done((bf16[192,65,1,128]{3,0,2,1:T(8,128)(2,1)S(1)}, bf16[192,65,1,128]{3,0,2,1:T(8,128)(2,1)S(1)}, u32[]{:S(2)}, u32[]{:S(2)}) %collective-permute-start.13) | collective-permute-done | bytes 3194912 | tf_op jit(solution)/shard_map/ppermute | solution.py:17
  762.8 6.3 add_reduce_fusion.5
  769.5 60.6 %psum.46 = f32[2,192,8]{1,2,0:T(8,128)S(1)} all-reduce(f32[2,192,8]{1,2,0:T(8,128)S(1)} %maximum_reduce_fusion), channel_id=1, replica_groups=mesh['batch'=2,'w'=4,'h'=4] {'h','w'}, use_global_device_ids=true, to_apply=%region_19.20 | all-reduce | flops 3072 | bytes 24576 | tf_op jit(solution)/shard_map/psum | solution.py:52
  830.5 3.8 maximum_convert_fusion.5
  837.0 6.4 collective-permute-done.15
  846.7 68.6 %collective-permute-done.16 = bf16[192,34,1,256]{3,0,2,1:T(8,128)(2,1)S(1)} collective-permute-done((bf16[192,34,1,256]{3,0,2,1:T(8,128)(2,1)S(1)}, bf16[192,34,1,256]{3,0,2,1:T(8,128)(2,1)S(1)}, u32[]{:S(2)}, u32[]{:S(2)}) %collective-permute-start.16) | collective-permute-done | bytes 3342368 | tf_op jit(solution)/shard_map/ppermute | solution.py:17
  915.3 4.9 collective-permute-done.17
  920.2 10.1 %add_reduce_fusion.4 = (f32[192,256]{1,0:T(8,128)S(1)}, f32[192,256]{1,0:T(8,128)S(1)}, f32[192,32,1,256]{3,0,2,1:T(8,128)}) fusion(f32[256]{0:T(256)S(1)} %bitcast.205, bf16[3,3,256,256]{3,2,1,0:T(8,128)(2,1)S(1)} %copy-done, bf16[192,34,1,256]{3,0,2,1:T(8,128)(2,1)S(1)} %collective-permute-done.17, ...), kind=kOutput, calls=%fused_computation.59 | convolution fusion | flops 7274004480 | bytes 17892352 | tf_op jit(solution)/shard_map/conv_general_dilated | solution.py:46
  930.7 58.7 %psum.47 = f32[2,192,8]{1,2,0:T(8,128)S(1)} all-reduce(f32[2,192,8]{1,2,0:T(8,128)S(1)} %maximum_reduce_fusion.1), channel_id=1, replica_groups=mesh['batch'=2,'w'=4,'h'=4] {'h','w'}, use_global_device_ids=true, to_apply=%region_23.24 | all-reduce | flops 3072 | bytes 24576 | tf_op jit(solution)/shard_map/psum | solution.py:52
  (108 shorter events, 53.3 us)
Async XLA Ops:
  0.0 920.2 %copy-start = (bf16[3,3,256,256]{3,2,1,0:T(8,128)(2,1)S(1)}, bf16[3,3,256,256]{3,2,1,0:T(8,128)(2,1)}, u32[]{:S(2)}) copy-start(bf16[3,3,256,256]{3,2,1,0:T(8,128)(2,1)} %param.24) | copy-start | bytes 3538948
  4.6 3.2 collective-permute-start
  8.3 10.2 %collective-permute-start.1 = (bf16[192,257,1,1]{0,3,2,1:T(2,128)(2,1)S(1)}, bf16[192,257,1,1]{0,3,2,1:T(2,128)(2,1)S(1)}, u32[]{:S(2)}, u32[]{:S(2)}) collective-permute-start(bf16[192,257,1,1]{0,3,2,1:T(2,128)(2,1)S(1)} %pad_maximum_fusion.7), channel_id=1, source_target_pairs={{0,4},{4,8},{8,12},{1,5},{5,9},{9,13},{2,6},{6,10},{10,14},{3,7},{... | collective-permute-start | bytes 296072 | tf_op jit(solution)/shard_map/ppermute | solution.py:17
  111.2 2.8 collective-permute-start.2
  112.5 13.2 %copy-start.4 = (f32[3,64]{1,0:T(4,128)S(1)}, f32[3,64]{1,0:T(4,128)}, u32[]{:S(2)}) copy-start(f32[3,64]{1,0:T(4,128)} %param.17) | copy-start | bytes 2308
  112.5 108.2 %copy-start.11 = (bf16[3,3,64,64]{3,2,1,0:T(8,128)(2,1)S(1)}, bf16[3,3,64,64]{3,2,1,0:T(8,128)(2,1)}, u32[]{:S(2)}) copy-start(bf16[3,3,64,64]{3,2,1,0:T(8,128)(2,1)} %param.16) | copy-start | bytes 221188
  112.5 7.4 collective-permute-start.3
  122.8 90.8 %collective-permute-start.4 = (bf16[192,130,1,64]{0,3,2,1:T(8,128)(2,1)S(1)}, bf16[192,130,1,64]{0,3,2,1:T(8,128)(2,1)S(1)}, u32[]{:S(2)}, u32[]{:S(2)}) collective-permute-start(bf16[192,130,1,64]{0,3,2,1:T(8,128)(2,1)S(1)} %get-tuple-element.29), channel_id=1, source_target_pairs={{0,4},{4,8},{8,12},{1,5},{5,9},{9,13},{2,6},{6,10},{10,14},{3,7},{... | collective-permute-start | bytes 9584648 | tf_op jit(solution)/shard_map/ppermute | solution.py:17
  124.4 94.2 %collective-permute-start.5 = (bf16[192,130,1,64]{0,3,2,1:T(8,128)(2,1)S(1)}, bf16[192,130,1,64]{0,3,2,1:T(8,128)(2,1)S(1)}, u32[]{:S(2)}, u32[]{:S(2)}) collective-permute-start(bf16[192,130,1,64]{0,3,2,1:T(8,128)(2,1)S(1)} %get-tuple-element.30), channel_id=1, source_target_pairs={{4,0},{8,4},{12,8},{5,1},{9,5},{13,9},{6,2},{10,6},{14,10},{7,3},{... | collective-permute-start | bytes 9584648 | tf_op jit(solution)/shard_map/ppermute | solution.py:17
  218.6 2.1 copy-start.7
  330.2 4.9 copy-start.5
  330.2 95.2 %copy-start.12 = (bf16[3,3,64,128]{3,2,1,0:T(8,128)(2,1)S(1)}, bf16[3,3,64,128]{3,2,1,0:T(8,128)(2,1)}, u32[]{:S(2)}) copy-start(bf16[3,3,64,128]{3,2,1,0:T(8,128)(2,1)} %param.18) | copy-start | bytes 442372
  330.2 2.4 collective-permute-start.6
  333.3 90.2 %collective-permute-start.7 = (bf16[192,129,1,64]{0,3,2,1:T(8,128)(2,1)S(1)}, bf16[192,129,1,64]{0,3,2,1:T(8,128)(2,1)S(1)}, u32[]{:S(2)}, u32[]{:S(2)}) collective-permute-start(bf16[192,129,1,64]{0,3,2,1:T(8,128)(2,1)S(1)} %pad_maximum_fusion.4), channel_id=1, source_target_pairs={{0,4},{4,8},{8,12},{1,5},{5,9},{9,13},{2,6},{6,10},{10,14},{3,7},{... | collective-permute-start | bytes 9510920 | tf_op jit(solution)/shard_map/ppermute | solution.py:17
  512.6 2.6 collective-permute-start.8
  513.9 8.3 collective-permute-start.9
  522.2 80.0 %slice-start = ((s8[6291456]{0:T(1024)(128)(4,1)}), s8[4194304]{0:T(1024)(128)(4,1)S(1)}, s32[]{:S(2)}) async-start(s8[6291456]{0:T(1024)(128)(4,1)} %bitcast.191), calls=%async_computation | async-start | bytes 8388608
  526.4 4.6 copy-start.6
  526.4 75.8 %slice-start.1 = ((s8[6291456]{0:T(1024)(128)(4,1)}), s8[2097152]{0:T(1024)(128)(4,1)S(1)}, s32[]{:S(2)}) async-start(s8[6291456]{0:T(1024)(128)(4,1)} %bitcast.191), calls=%async_computation.1 | async-start | bytes 4194304
  526.5 75.8 %copy-start.10 = (bf16[3,3,128,128]{3,2,1,0:T(8,128)(2,1)S(1)}, bf16[3,3,128,128]{3,2,1,0:T(8,128)(2,1)}, u32[]{:S(2)}) copy-start(bf16[3,3,128,128]{3,2,1,0:T(8,128)(2,1)} %param.20) | copy-start | bytes 884740
  528.0 69.3 %collective-permute-start.10 = (bf16[192,66,1,128]{3,0,2,1:T(8,128)(2,1)S(1)}, bf16[192,66,1,128]{3,0,2,1:T(8,128)(2,1)S(1)}, u32[]{:S(2)}, u32[]{:S(2)}) collective-permute-start(bf16[192,66,1,128]{3,0,2,1:T(8,128)(2,1)S(1)} %get-tuple-element.33), channel_id=1, source_target_pairs={{0,4},{4,8},{8,12},{1,5},{5,9},{9,13},{2,6},{6,10},{10,14},{3,7},{... | collective-permute-start | bytes 9732104 | tf_op jit(solution)/shard_map/ppermute | solution.py:17
  529.5 72.7 %collective-permute-start.11 = (bf16[192,66,1,128]{3,0,2,1:T(8,128)(2,1)S(1)}, bf16[192,66,1,128]{3,0,2,1:T(8,128)(2,1)S(1)}, u32[]{:S(2)}, u32[]{:S(2)}) collective-permute-start(bf16[192,66,1,128]{3,0,2,1:T(8,128)(2,1)S(1)} %get-tuple-element.34), channel_id=1, source_target_pairs={{4,0},{8,4},{12,8},{5,1},{9,5},{13,9},{6,2},{10,6},{14,10},{7,3},{... | collective-permute-start | bytes 9732104 | tf_op jit(solution)/shard_map/ppermute | solution.py:17
  688.5 7.4 copy-start.2
  688.5 74.3 %copy-start.1 = (bf16[192,64,2,128]{3,0,2,1:T(8,128)(2,1)S(1)}, bf16[192,64,2,128]{3,0,2,1:T(8,128)(2,1)}, u32[]{:S(2)}) copy-start(bf16[192,64,2,128]{3,0,2,1:T(8,128)(2,1)} %maximum_convert_fusion.2) | copy-start | bytes 18874372
  688.5 74.3 %copy-start.9 = (bf16[3,3,128,256]{3,2,1,0:T(8,128)(2,1)S(1)}, bf16[3,3,128,256]{3,2,1,0:T(8,128)(2,1)}, u32[]{:S(2)}) copy-start(bf16[3,3,128,256]{3,2,1,0:T(8,128)(2,1)} %param.22) | copy-start | bytes 1769476
  689.5 2.5 collective-permute-start.12
  694.2 68.6 %collective-permute-start.13 = (bf16[192,65,1,128]{3,0,2,1:T(8,128)(2,1)S(1)}, bf16[192,65,1,128]{3,0,2,1:T(8,128)(2,1)S(1)}, u32[]{:S(2)}, u32[]{:S(2)}) collective-permute-start(bf16[192,65,1,128]{3,0,2,1:T(8,128)(2,1)S(1)} %pad_maximum_fusion.6), channel_id=1, source_target_pairs={{0,4},{4,8},{8,12},{1,5},{5,9},{9,13},{2,6},{6,10},{10,14},{3,7},{... | collective-permute-start | bytes 9584648 | tf_op jit(solution)/shard_map/ppermute | solution.py:17
  830.5 16.2 %copy-start.3 = (f32[3,256]{1,0:T(4,128)S(1)}, f32[3,256]{1,0:T(4,128)}, u32[]{:S(2)}) copy-start(f32[3,256]{1,0:T(4,128)} %param.25) | copy-start | bytes 9220
  834.4 2.6 collective-permute-start.14
  835.7 7.8 collective-permute-start.15
  843.9 71.4 %collective-permute-start.16 = (bf16[192,34,1,256]{3,0,2,1:T(8,128)(2,1)S(1)}, bf16[192,34,1,256]{3,0,2,1:T(8,128)(2,1)S(1)}, u32[]{:S(2)}, u32[]{:S(2)}) collective-permute-start(bf16[192,34,1,256]{3,0,2,1:T(8,128)(2,1)S(1)} %pad_maximum_fusion.5), channel_id=1, source_target_pairs={{0,4},{4,8},{8,12},{1,5},{5,9},{9,13},{2,6},{6,10},{10,14},{3,7},{... | collective-permute-start | bytes 10027016 | tf_op jit(solution)/shard_map/ppermute | solution.py:17
  845.4 74.8 %collective-permute-start.17 = (bf16[192,34,1,256]{3,0,2,1:T(8,128)(2,1)S(1)}, bf16[192,34,1,256]{3,0,2,1:T(8,128)(2,1)S(1)}, u32[]{:S(2)}, u32[]{:S(2)}) collective-permute-start(bf16[192,34,1,256]{3,0,2,1:T(8,128)(2,1)S(1)} %pad_maximum_fusion.5), channel_id=1, source_target_pairs={{4,0},{8,4},{12,8},{5,1},{9,5},{13,9},{6,2},{10,6},{14,10},{7,3},{... | collective-permute-start | bytes 10027016 | tf_op jit(solution)/shard_map/ppermute | solution.py:17
  (1 other events, 2.0 us)
where the time goes:
time: 1010 us; the launch traced here: 998 us
  waiting for transfers between devices  420 us (42%)
  blocking collectives  358 us (35%)
  matrix products  104 us (10%)
  other arithmetic  66.6 us (7%)
  starting transfers between devices  29.7 us (3%)
  local copies, waits for them, and re-layouts  18.3 us (2%)
    ppermute x18, waiting for transfers between devices, shift_in(): return lax.ppermute(piece, axis_name, send_pairs)  420 us
    psum x6, blocking collectives, conv_norm(): totals = lax.psum(part_sums, ('h', 'w'))  358 us
    conv_general_dilated x6, matrix products, conv_norm(): lax.conv_general_dilated(padded, kernel, (stride, stride), 'VALID', dimen...  104 us
    convert_element_type x6, other arithmetic, norm_apply(): jax.nn.relu(summed * chan_scale[:, None, None, :] + chan_shift[:, None, N...  54.7 us
    ppermute x18, starting transfers between devices, shift_in(): return lax.ppermute(piece, axis_name, send_pairs)  29.7 us
  transfers between devices with their start and end apart: 18, of which 15 were waited for; matrix products, arithmetic and copies ran while one was open for 0% of the time, Pallas kernels for 0%

commit v1 on v0

v1 whole, which is shorter than its diff:
```python
import jax
import jax.numpy as jnp
from jax import lax
from jax.sharding import PartitionSpec as P

NORM_GROUPS = 8
NORM_EPS = 1e-5


def conv_norm(inputs, kernel, affine, stride):
    summed = lax.conv_general_dilated(inputs, kernel, (stride, stride), ((1, 1), (1, 1)), dimension_numbers=("NHWC", "HWIO", "NHWC"), preferred_element_type=jnp.float32) + affine[0]
    out_shape = summed.shape
    per_group = out_shape[3] // NORM_GROUPS
    pixel_count = out_shape[1] * out_shape[2] * per_group
    part_sums = jnp.stack([jnp.sum(summed, axis=(1, 2)), jnp.sum(jnp.square(summed), axis=(1, 2))])
    totals = jnp.sum(part_sums.reshape(2, out_shape[0], NORM_GROUPS, per_group), axis=3)
    grp_mean = totals[0] / pixel_count
    grp_var = jnp.maximum(totals[1] / pixel_count - jnp.square(grp_mean), 0.0)
    inv_std = lax.rsqrt(grp_var + NORM_EPS)
    chan_scale = jnp.repeat(inv_std, per_group, axis=1) * affine[1]
    chan_shift = affine[2] - jnp.repeat(grp_mean * inv_std, per_group, axis=1) * affine[1]
    return jax.nn.relu(summed * chan_scale[:, None, None, :] + chan_shift[:, None, None, :]).astype(jnp.bfloat16)


def solution(mesh):
    rows = mesh.shape["h"]
    cols = mesh.shape["w"]
    act_spec = P("batch", "h", "w")

    def local_forward(tile, *params):
        count, height, width, _ = tile.shape
        share = count // (rows * cols)
        sent = tile.reshape(rows * cols, share, height, width)
        got = lax.all_to_all(sent, ("h", "w"), 0, 0, tiled=True)
        got = got.reshape(rows, cols, share, height, width)
        current = got.transpose(2, 0, 3, 1, 4).reshape(share, rows * height, cols * width, 1)
        for stage in range(3):
            down_w, down_v, refine_w, refine_v = params[4 * stage:4 * stage + 4]
            current = conv_norm(current, down_w, down_v, 2)
            current = conv_norm(current, refine_w, refine_v, 1)
        chan = current.shape[3]
        out_h = current.shape[1] // rows
        out_w = current.shape[2] // cols
        back = current.reshape(share, rows, out_h, cols, out_w, chan).transpose(1, 3, 0, 2, 4, 5)
        back = back.reshape(rows * cols, share, out_h, out_w, chan)
        back = lax.all_to_all(back, ("h", "w"), 0, 0, tiled=True)
        return back.reshape(count, out_h, out_w, chan)

    return jax.shard_map(local_forward, mesh=mesh, in_specs=(act_spec,) + (P(),) * 12, out_specs=act_spec, check_vma=False)
```

time: 1010 us -> 343 us (0.34)
  waiting for transfers between devices: 420 us -> 15.4 us
  blocking collectives: 358 us -> 76.7 us
  matrix products: 104 us -> 195 us
  other arithmetic: 66.6 us -> 5.61 us
  starting transfers between devices: 29.7 us -> 7.58 us
  local copies, waits for them, and re-layouts: 18.3 us -> 35.8 us
    ppermute x18 -> x0, waiting for transfers between devices: 420 us -> none  [shift_in(): return lax.ppermute(piece, axis_name, send_pairs)]
    psum x6 -> x0, blocking collectives: 358 us -> none  [conv_norm(): totals = lax.psum(part_sums, ('h', 'w'))]
    conv_general_dilated x6, matrix products: 104 us -> 195 us  [conv_norm(): lax.conv_general_dilated(inputs, kernel, (stride, stride), ((1, 1), (1, 1...]
    all_to_all x0 -> x1, blocking collectives: none -> 76.7 us  [local_forward(): back = lax.all_to_all(back, ('h', 'w'), 0, 0, tiled=True)]
    convert_element_type x6 -> x1, other arithmetic: 54.7 us -> 4.88 us  [conv_norm(): jax.nn.relu(summed * chan_scale[:, None, None, :] + chan_shift[:, None, N...]
    ppermute x18 -> x0, starting transfers between devices: 29.7 us -> none  [shift_in(): return lax.ppermute(piece, axis_name, send_pairs)]
    reshape x0 -> x15, local copies, waits for them, and re-layouts: none -> 24 us  [the longest x2 21.1 us: local_forward(): got.transpose(2, 0, 3, 1, 4).reshape(share, rows * height, cols * width, 1)]
    all_to_all x0 -> x1, waiting for transfers between devices: none -> 15.4 us  [local_forward(): got = lax.all_to_all(sent, ('h', 'w'), 0, 0, tiled=True)]
  transfers between devices with their start and end apart: 18 -> 1, of which waited for: 15 -> 1; matrix products, arithmetic and copies ran while one was open for 0% -> 2% of each run, Pallas kernels for 0% -> 0%
where the time goes in v1:
time: 343 us; the launch traced here: 337 us
  matrix products  195 us (57%)
  blocking collectives  76.7 us (22%)
  local copies, waits for them, and re-layouts  35.8 us (10%)
  waiting for transfers between devices  15.4 us (4%)
  starting transfers between devices  7.58 us (2%)
  other arithmetic  5.61 us (2%)
    conv_general_dilated x6, matrix products, conv_norm(): lax.conv_general_dilated(inputs, kernel, (stride, stride), ((1, 1), (1, 1...  195 us
    all_to_all x1, blocking collectives, local_forward(): back = lax.all_to_all(back, ('h', 'w'), 0, 0, tiled=True)  76.7 us
    reshape x2, local copies, waits for them, and re-layouts, local_forward(): got.transpose(2, 0, 3, 1, 4).reshape(share, rows * height, cols * width, 1)  21.1 us
    all_to_all x1, waiting for transfers between devices, local_forward(): got = lax.all_to_all(sent, ('h', 'w'), 0, 0, tiled=True)  15.4 us
    all_to_all x1, starting transfers between devices, local_forward(): got = lax.all_to_all(sent, ('h', 'w'), 0, 0, tiled=True)  7.58 us
  transfers between devices with their start and end apart: 1, of which 1 were waited for; matrix products, arithmetic and copies ran while one was open for 2% of the time, Pallas kernels for 0%

profile of v1, /device:TPU:0, one launch (start us, length us, event | category | flops | bytes accessed | tf_op | source)
XLA Modules:
  0.0 336.7 jit_solution(15992797218735573482)
XLA Ops:
  0.0 7.6 %all-to-all-start = ((bf16[16,12,256,8]{2,3,1,0:T(8,128)(2,1)}), bf16[16,12,256,8]{2,3,1,0:T(8,128)(2,1)S(1)}, u32[]{:S(2)}, u32[]{:S(2)}) async-start(bf16[16,12,256,8]{2,3,1,0:T(8,128)(2,1)} %bitcast.158), calls=%async_computation | async-start | bytes 1572864 | tf_op jit(solution)/shard_map/all_to_all | solution.py:34
  7.6 1.4 fusion.59
  9.0 1.4 fusion.58
  10.4 1.3 slice_bitcast_fusion.7
  11.7 1.5 slice_bitcast_fusion.1
  13.2 15.4 %all-to-all-done = bf16[16,12,256,8]{2,3,1,0:T(8,128)(2,1)S(1)} async-done(((bf16[16,12,256,8]{2,3,1,0:T(8,128)(2,1)}), bf16[16,12,256,8]{2,3,1,0:T(8,128)(2,1)S(1)}, u32[]{:S(2)}, u32[]{:S(2)}) %all-to-all-start) | async-done | bytes 786464 | tf_op jit(solution)/shard_map/all_to_all | solution.py:34
  28.6 0.6 copy.96
  29.2 0.6 reshape.398
  29.7 20.6 %copy.97 = bf16[12,1024,32,1]{0,3,2,1:T(2,128)(2,1)} copy(bf16[12,1024,32,1]{1,2,0,3:T(8,128)(2,1)S(1)} %reshape.398) | data formatting | bytes 1572864 | tf_op jit(solution)/shard_map/reshape | solution.py:36
  50.3 49.5 %add_reduce_fusion.1 = (f32[12,64]{1,0:T(8,128)S(1)}, f32[12,64]{1,0:T(8,128)S(1)}, f32[12,512,16,64]{3,0,2,1:T(8,128)}) fusion(f32[64]{0:T(128)S(1)} %get-tuple-element.78, bf16[12,1024,32,1]{0,3,2,1:T(2,128)(2,1)} %copy.97, bf16[3,3,1,64]{3,1,2,0:T(4,128)(2,1)S(1)} %copy-done.19), kind=kOutput, calls=%fused_computation.5 | convolution fusion | flops 135979008 | bytes 25959808 | tf_op jit(solution)/shard_map/conv_general_dilated | solution.py:11
  100.0 0.1 maximum_reduce_fusion
  100.7 0.1 reshape.400
  100.8 61.0 %add_reduce_fusion = (f32[12,64]{1,0:T(8,128)S(1)}, f32[12,64]{1,0:T(8,128)S(1)}, f32[12,512,16,64]{3,0,2,1:T(8,128)}) fusion(f32[64]{0:T(128)S(1)} %get-tuple-element.54, bf16[3,3,64,64]{3,2,1,0:T(8,128)(2,1)S(1)} %copy-done.17, f32[12,512,16,64]{3,0,2,1:T(8,128)} %get-tuple-element.71, f32[12,64]{1,0:T(8,128)S(1)} %get-tuple-element.70, ...), kind=kOutput, calls=%fused_computation.4 | convolution fusion | flops 6993344512 | bytes 50418176 | tf_op jit(solution)/shard_map/conv_general_dilated | solution.py:11
  162.0 0.1 maximum_reduce_fusion.1
  162.7 0.1 reshape.402
  162.9 30.8 %add_reduce_fusion.3 = (f32[12,128]{1,0:T(8,128)S(1)}, f32[12,128]{1,0:T(8,128)S(1)}, f32[12,256,8,128]{3,0,2,1:T(8,128)}) fusion(f32[128]{0:T(128)S(1)} %copy-done.14, bf16[3,3,64,128]{3,2,1,0:T(8,128)(2,1)S(1)} %copy-done.18, f32[12,512,16,64]{3,0,2,1:T(8,128)} %get-tuple-element.72, f32[12,64]{1,0:T(8,128)S(1)} %get-tuple-element.68, ...), kind=kOutput, calls=%fused_computation.17 | convolution fusion | flops 3512398848 | bytes 37915392 | tf_op jit(solution)/shard_map/conv_general_dilated | solution.py:11
  193.9 0.1 maximum_reduce_fusion.2
  194.6 0.1 reshape.404
  194.8 24.9 %add_reduce_fusion.2 = (f32[12,128]{1,0:T(8,128)S(1)}, f32[12,128]{1,0:T(8,128)S(1)}, f32[12,256,8,128]{3,0,2,1:T(8,128)}) fusion(f32[128]{0:T(128)S(1)} %copy-done.13, bf16[3,3,128,128]{3,2,1,0:T(8,128)(2,1)S(1)} %copy-done.16, f32[12,256,8,128]{3,0,2,1:T(8,128)} %get-tuple-element.73, f32[12,128]{1,0:T(8,128)S(1)} %get-tuple-element.66, ...), kind=kOutput, calls=%fused_computation.16 | convolution fusion | flops 6654784512 | bytes 25486336 | tf_op jit(solution)/shard_map/conv_general_dilated | solution.py:11
  219.9 0.1 maximum_reduce_fusion.3
  220.5 0.1 reshape.406
  220.7 12.6 %add_reduce_fusion.5 = (f32[12,256]{1,0:T(8,128)S(1)}, f32[12,256]{1,0:T(8,128)S(1)}, f32[12,128,4,256]{3,0,2,1:T(8,128)}) fusion(f32[256]{0:T(256)S(1)} %bitcast.165, bf16[3,3,128,256]{3,2,1,0:T(8,128)(2,1)S(1)} %copy-done.15, f32[12,256,8,128]{3,0,2,1:T(8,128)} %get-tuple-element.74, f32[12,128]{1,0:T(8,128)S(1)} %get-tuple-element.64, ...), kind=kOutput, calls=%fused_computation.33 | convolution fusion | flops 3335251968 | bytes 19502592 | tf_op jit(solution)/shard_map/conv_general_dilated | solution.py:11
  233.5 0.1 maximum_reduce_fusion.4
  234.0 0.1 reshape.407
  234.2 0.1 reshape.408
  234.4 15.7 %add_reduce_fusion.4 = (f32[12,256]{1,0:T(8,128)S(1)}, f32[12,256]{1,0:T(8,128)S(1)}, f32[12,128,4,256]{3,0,2,1:T(8,128)}) fusion(f32[256]{0:T(256)S(1)} %bitcast.159, bf16[3,3,256,256]{3,2,1,0:T(8,128)(2,1)S(1)} %copy-done, f32[12,128,4,256]{3,0,2,1:T(8,128)} %get-tuple-element.75, f32[12,256]{1,0:T(8,128)S(1)} %get-tuple-element.62, ...), kind=kOutput, calls=%fused_computation.32 | convolution fusion | flops 6022490112 | bytes 13813760 | tf_op jit(solution)/shard_map/conv_general_dilated | solution.py:11
  250.2 0.1 maximum_reduce_fusion.5
  250.9 0.1 reshape.410
  251.1 4.9 %maximum_convert_fusion.8 = bf16[12,128,4,256]{3,0,2,1:T(8,128)(2,1)S(1)} fusion(f32[12,128,4,256]{3,0,2,1:T(8,128)} %get-tuple-element.76, f32[12,256]{1,0:T(8,128)S(1)} %get-tuple-element.60, f32[12,256]{1,0:T(8,128)S(1)} %get-tuple-element.59, f32[256]{0:T(256)S(1)} %bitcast.160), kind=kLoop, calls=%fused_computation.20 | loop fusion | flops 7864320 | bytes 9462784 | tf_op jit(solution)/shard_map/convert_element_type | solution.py:22
  256.0 1.8 copy.123
  257.8 76.7 %all_to_all.10 = bf16[16,12,32,1,256]{4,2,1,3,0:T(8,128)(2,1)S(1)} all-to-all(bf16[16,12,32,1,256]{4,2,1,3,0:T(8,128)(2,1)S(1)} %bitcast.155), channel_id=1, replica_groups=mesh['batch'=2,'w'=4,'h'=4] {'h','w'}, dimensions={0} | all-to-all | bytes 6291456 | tf_op jit(solution)/shard_map/all_to_all | solution.py:46
  334.5 1.7 copy.143
  (111 shorter events, 4.4 us)
Async XLA Ops:
  0.0 234.3 %copy-start = (bf16[3,3,256,256]{3,2,1,0:T(8,128)(2,1)S(1)}, bf16[3,3,256,256]{3,2,1,0:T(8,128)(2,1)}, u32[]{:S(2)}) copy-start(bf16[3,3,256,256]{3,2,1,0:T(8,128)(2,1)} %param.24) | copy-start | bytes 3538948
  0.0 50.3 %copy-start.19 = (bf16[3,3,1,64]{3,1,2,0:T(4,128)(2,1)S(1)}, bf16[3,3,1,64]{3,1,2,0:T(4,128)(2,1)}, u32[]{:S(2)}) copy-start(bf16[3,3,1,64]{3,1,2,0:T(4,128)(2,1)} %param.14) | copy-start | bytes 3460
  0.0 28.6 %all-to-all-start = ((bf16[16,12,256,8]{2,3,1,0:T(8,128)(2,1)}), bf16[16,12,256,8]{2,3,1,0:T(8,128)(2,1)S(1)}, u32[]{:S(2)}, u32[]{:S(2)}) async-start(bf16[16,12,256,8]{2,3,1,0:T(8,128)(2,1)} %bitcast.158), calls=%async_computation | async-start | bytes 1572864 | tf_op jit(solution)/shard_map/all_to_all | solution.py:34
  50.3 50.5 %copy-start.17 = (bf16[3,3,64,64]{3,2,1,0:T(8,128)(2,1)S(1)}, bf16[3,3,64,64]{3,2,1,0:T(8,128)(2,1)}, u32[]{:S(2)}) copy-start(bf16[3,3,64,64]{3,2,1,0:T(8,128)(2,1)} %param.16) | copy-start | bytes 221188
  100.8 62.0 %copy-start.10 = (f32[64]{0:T(128)S(1)}, f32[64]{0:T(128)}, u32[]{:S(2)}) copy-start(f32[64]{0:T(128)} %get-tuple-element.53) | copy-start | bytes 772
  100.8 62.0 %copy-start.11 = (f32[64]{0:T(128)S(1)}, f32[64]{0:T(128)}, u32[]{:S(2)}) copy-start(f32[64]{0:T(128)} %get-tuple-element.55) | copy-start | bytes 772
  100.8 62.1 %copy-start.14 = (f32[128]{0:T(128)S(1)}, f32[128]{0:T(128)}, u32[]{:S(2)}) copy-start(f32[128]{0:T(128)} %get-tuple-element.81) | copy-start | bytes 1540
  100.8 62.1 %copy-start.18 = (bf16[3,3,64,128]{3,2,1,0:T(8,128)(2,1)S(1)}, bf16[3,3,64,128]{3,2,1,0:T(8,128)(2,1)}, u32[]{:S(2)}) copy-start(bf16[3,3,64,128]{3,2,1,0:T(8,128)(2,1)} %param.18) | copy-start | bytes 442372
  162.9 31.8 %copy-start.8 = (f32[128]{0:T(128)S(1)}, f32[128]{0:T(128)}, u32[]{:S(2)}) copy-start(f32[128]{0:T(128)} %get-tuple-element.80) | copy-start | bytes 1540
  162.9 31.8 %copy-start.9 = (f32[128]{0:T(128)S(1)}, f32[128]{0:T(128)}, u32[]{:S(2)}) copy-start(f32[128]{0:T(128)} %get-tuple-element.82) | copy-start | bytes 1540
  162.9 31.9 %copy-start.13 = (f32[128]{0:T(128)S(1)}, f32[128]{0:T(128)}, u32[]{:S(2)}) copy-start(f32[128]{0:T(128)} %get-tuple-element.48) | copy-start | bytes 1540
  162.9 31.9 %copy-start.16 = (bf16[3,3,128,128]{3,2,1,0:T(8,128)(2,1)S(1)}, bf16[3,3,128,128]{3,2,1,0:T(8,128)(2,1)}, u32[]{:S(2)}) copy-start(bf16[3,3,128,128]{3,2,1,0:T(8,128)(2,1)} %param.20) | copy-start | bytes 884740
  194.8 25.9 %copy-start.6 = (f32[128]{0:T(128)S(1)}, f32[128]{0:T(128)}, u32[]{:S(2)}) copy-start(f32[128]{0:T(128)} %get-tuple-element.47) | copy-start | bytes 1540
  194.8 25.9 %copy-start.7 = (f32[128]{0:T(128)S(1)}, f32[128]{0:T(128)}, u32[]{:S(2)}) copy-start(f32[128]{0:T(128)} %get-tuple-element.49) | copy-start | bytes 1540
  194.8 25.9 %copy-start.12 = (f32[1,256]{1,0:T(1,128)S(1)}, f32[1,256]{1,0:T(1,128)}, u32[]{:S(2)}) copy-start(f32[1,256]{1,0:T(1,128)} %get-tuple-element.45) | copy-start | bytes 3076
  194.8 25.9 %copy-start.15 = (bf16[3,3,128,256]{3,2,1,0:T(8,128)(2,1)S(1)}, bf16[3,3,128,256]{3,2,1,0:T(8,128)(2,1)}, u32[]{:S(2)}) copy-start(bf16[3,3,128,256]{3,2,1,0:T(8,128)(2,1)} %param.22) | copy-start | bytes 1769476
  220.7 13.6 %copy-start.4 = (f32[1,256]{1,0:T(1,128)S(1)}, f32[1,256]{1,0:T(1,128)}, u32[]{:S(2)}) copy-start(f32[1,256]{1,0:T(1,128)} %get-tuple-element.44) | copy-start | bytes 3076
  220.7 13.6 %copy-start.5 = (f32[1,256]{1,0:T(1,128)S(1)}, f32[1,256]{1,0:T(1,128)}, u32[]{:S(2)}) copy-start(f32[1,256]{1,0:T(1,128)} %get-tuple-element.46) | copy-start | bytes 3076
  220.7 13.6 %copy-start.1 = (f32[1,256]{1,0:T(1,128)S(1)}, f32[1,256]{1,0:T(1,128)}, u32[]{:S(2)}) copy-start(f32[1,256]{1,0:T(1,128)} %get-tuple-element.42) | copy-start | bytes 3076
  234.4 16.7 %copy-start.2 = (f32[1,256]{1,0:T(1,128)S(1)}, f32[1,256]{1,0:T(1,128)}, u32[]{:S(2)}) copy-start(f32[1,256]{1,0:T(1,128)} %get-tuple-element.41) | copy-start | bytes 3076
  234.4 16.7 %copy-start.3 = (f32[1,256]{1,0:T(1,128)S(1)}, f32[1,256]{1,0:T(1,128)}, u32[]{:S(2)}) copy-start(f32[1,256]{1,0:T(1,128)} %get-tuple-element.43) | copy-start | bytes 3076

commit v2 on v1

v2 whole, which is shorter than its diff:
```python
import jax
import jax.numpy as jnp
from jax import lax
from jax.experimental import pallas as pl
from jax.experimental.pallas import tpu as pltpu
from jax.sharding import PartitionSpec as P

NORM_EPS = 1e-5
LANE = 128
BLOCK = 256
WIDE = 1024
BF = jnp.bfloat16
F32 = jnp.float32
MESH = pl.DeviceIdType.MESH
ROWS = (8, 8, 4, 4, 2, 2)
CHANS = (64, 64, 128, 128, 256, 256)


def iota(shape, axis):
    return lax.broadcasted_iota(jnp.int32, shape, axis)


def make_kernel(share):
    chunks = share // 4

    def kernel(x_ref, w1d, v1d, w1r, v1r, w2d, v2d, w2r, v2r, w3d, v3d, w3r, v3r, o_ref,
               slab, recv, ze, zo, t1, tr1, td2, tr2, aff, gmat, smat, pmat,
               acc, zd1, zr1, zd2, zr2, zd3, fst, outb,
               send_in, recv_in, send_out, recv_out, local_out):
        wi = lax.axis_index("w")
        hi = lax.axis_index("h")
        me = hi * 4 + wi
        barrier = pltpu.get_barrier_semaphore()

        def peer(k):
            d = lax.rem(me + k, 16)
            return d, {"h": d // 4, "w": lax.rem(d, 4)}

        for k in range(1, 16):
            pl.semaphore_signal(barrier, inc=1, device_id=peer(k)[1], device_id_type=MESH)

        r, c = iota((BLOCK, BLOCK), 0), iota((BLOCK, BLOCK), 1)
        half, parity, quarter, strip = r // LANE, (r // 64) % 2, (r // 16) % 4, r % 16
        pmat[...] = (c == strip * 16 + half * 8 + quarter * 2 + parity).astype(F32).astype(BF)

        def pack(k, carry):
            d, _ = peer(k)
            rows = x_ref[pl.ds(pl.multiple_of(d * (8 * share), 32), 8 * share), :]
            turned = lax.dot_general(pmat[...], rows, (((1,), (1,)), ((), ())), preferred_element_type=F32).astype(BF)
            for ch in range(chunks):
                for q in range(4):
                    slab[ch, k, :, 32 * q:32 * q + 32] = turned[64 * q:64 * q + 64, 32 * ch:32 * ch + 32]
            return carry

        lax.fori_loop(0, 16, pack, 0)
        pl.semaphore_wait(barrier, 15)

        def in_copy(ch, k):
            _, dev = peer(k)
            return pltpu.make_async_remote_copy(
                src_ref=slab.at[ch, k], dst_ref=recv.at[ch, me], send_sem=send_in, recv_sem=recv_in.at[ch],
                device_id=dev, device_id_type=MESH)

        for ch in range(chunks):
            def send(k, carry, ch=ch):
                in_copy(ch, k).start()
                return carry
            lax.fori_loop(1, 16, send, 0)
            recv[ch, me] = slab[ch, 0]

        r, c = iota((512, 512), 0), iota((512, 512), 1)
        smat[...] = ((r // LANE == (c // 8) % 4) & ((r // 32) % 4 == c // LANE) & ((r // 8) % 4 == (c // 32) % 4)
                     & (r % 8 == c % 8)).astype(F32).astype(BF)
        r, c = iota((384, LANE), 0) % LANE, iota((384, LANE), 1)
        for s, chan in enumerate((64, LANE, BLOCK)):
            size = chan // 8
            gmat[s] = ((r % chan) // size == (c % chan) // size).astype(F32).astype(BF)
        for s, v in enumerate((v1d, v1r, v2d, v2r, v3d, v3r)):
            chan = CHANS[s]
            if chan == 64:
                aff[s, 0:3, :] = jnp.concatenate([v[...], v[...]], axis=1)
            else:
                aff[s, 0:3, :] = v[:, 0:LANE]
                if chan == BLOCK:
                    aff[s, 3:6, :] = v[:, LANE:BLOCK]
        t1[...] = jnp.zeros_like(t1)
        row, col = iota((32, WIDE), 0), iota((32, WIDE), 1) // 64
        for dh in range(3):
            base = jnp.zeros((32, WIDE), F32)
            for dw in range(3):
                tap = w1d[dh, dw:dw + 1, :].astype(F32)
                tap = jnp.concatenate([tap, tap], axis=1)
                tap = jnp.concatenate([tap] * 8, axis=1)
                base = jnp.where(row == 2 * col + dw - 1, jnp.broadcast_to(tap, (32, WIDE)), base)
            for i in range(4):
                t1[i, dh * LANE + 32 * i:dh * LANE + 32 * i + 32, :] = base.astype(BF)
        tr1[...] = jnp.zeros_like(tr1)
        td2[...] = jnp.zeros_like(td2)
        tr2[...] = jnp.zeros_like(tr2)
        for dh in range(3):
            for dw in range(3):
                tap = w1r[dh, 64 * dw:64 * dw + 64, :]
                for jo in range(4):
                    ji = jo + 1 + dw
                    tr1[dh, 64 * ji:64 * ji + 64, 64 * jo:64 * jo + 64] = tap
                tap = w2d[dh, 64 * dw:64 * dw + 64, :]
                for jo in range(2):
                    ji = 2 * jo + 1 + dw
                    td2[dh, 64 * ji:64 * ji + 64, LANE * jo:LANE * jo + LANE] = tap
                tap = w2r[dh, LANE * dw:LANE * dw + LANE, :]
                for jo in range(2):
                    ji = jo + dw
                    tr2[dh, LANE * ji:LANE * ji + LANE, LANE * jo:LANE * jo + LANE] = tap

        top = iota((64, BLOCK), 0) == 0
        bottom = iota((64, BLOCK), 0) == 63

        def taps(ref, j, rows, stride, lo, hi_):
            pieces = []
            for dh in range(3):
                if stride == 1:
                    piece = ref[j, :, dh:dh + rows, :, lo:hi_]
                    pieces.append(piece.reshape(64 * rows, hi_ - lo))
                else:
                    pieces.append(jnp.concatenate(
                        [ref[j, h, 2 * l + dh, :, lo:hi_] for h in range(4) for l in range(rows)], axis=0))
            return jnp.concatenate(pieces, axis=1)

        def conv(j, s, b, i):
            rows = ROWS[s]
            m = 64 * rows
            lo = BLOCK * b
            if s == 0:
                lhs = jnp.concatenate([zo[:, 0:8].reshape(m, LANE), ze[...].reshape(m, LANE),
                                       zo[:, 1:9].reshape(m, LANE)], axis=1)
                rhs = t1[i, :, lo:lo + BLOCK]
            elif s in (1, 3):
                ref, mat = ((zd1, tr1), (zd2, tr2))[s // 2]
                first, last = (LANE if b == 0 else 0), (384 if b == 3 else 512)
                lhs = taps(ref, j, rows, 1, lo - LANE + first, lo - LANE + last)
                rhs = mat[:, first:last, :].reshape(3 * (last - first), BLOCK)
            elif s in (2, 4):
                ref, mat = ((zr1, td2), (zr2, w3d))[s // 2 - 1]
                first = LANE if b == 0 else 0
                lhs = taps(ref, j, rows, 2, lo - LANE + first, lo + BLOCK)
                rhs = mat[:, first:384, :].reshape(3 * (384 - first), BLOCK)
            else:
                first, last = (BLOCK if b == 0 else 0), (512 if b == 3 else 768)
                lhs = taps(zd3, j, rows, 1, lo - BLOCK + first, lo - BLOCK + last)
                rhs = w3r[:, first:last, :].reshape(3 * (last - first), BLOCK)
            out = jnp.dot(lhs, rhs, preferred_element_type=F32)
            acc[j, 0:m, lo:lo + BLOCK] = out
            tall = out.reshape(m // 8, 8, BLOCK)
            return jnp.sum(tall, axis=0), jnp.sum(tall * tall, axis=0)

        def finish(s, parts):
            m, chan = 64 * ROWS[s], CHANS[s]
            sums = parts[0][0] + parts[1][0] + parts[2][0] + parts[3][0]
            sqs = parts[0][1] + parts[1][1] + parts[2][1] + parts[3][1]
            if chan == BLOCK:
                sides, per_lane = [(sums[:, 0:LANE], sqs[:, 0:LANE]), (sums[:, LANE:], sqs[:, LANE:])], 4.0 * m
            else:
                sides, per_lane = [(sums[:, 0:LANE] + sums[:, LANE:], sqs[:, 0:LANE] + sqs[:, LANE:])], 8.0 * m
            count = float(m * WIDE // 8)
            row16 = iota((16, LANE), 0)
            packed = jnp.zeros((16, LANE), F32)
            for n, (one, two) in enumerate(sides):
                bias = aff[s, 3 * n:3 * n + 1, :]
                one = jnp.sum(one, axis=0, keepdims=True)
                two = jnp.sum(two, axis=0, keepdims=True)
                total = one + per_lane * bias
                square = two + bias * (one + total)
                packed = jnp.where(row16 == 2 * n, total, jnp.where(row16 == 2 * n + 1, square, packed))
            high = packed.astype(BF)
            rest = packed - high.astype(F32)
            mid = rest.astype(BF)
            low = (rest - mid.astype(F32)).astype(BF)
            totals = jnp.dot(jnp.concatenate([high, mid, low], axis=1), gmat[s // 2], preferred_element_type=F32)
            scales, shifts = [], []
            for n in range(len(sides)):
                bias, gain, beta = (aff[s, 3 * n + t:3 * n + t + 1, :] for t in range(3))
                mean = totals[2 * n:2 * n + 1] * (1.0 / count)
                var = jnp.maximum(totals[2 * n + 1:2 * n + 2] * (1.0 / count) - mean * mean, 0.0)
                scale = lax.rsqrt(var + NORM_EPS) * gain
                scales.append(scale)
                shifts.append(beta + (bias - mean) * scale)
            if len(sides) == 1:
                scales, shifts = scales * 2, shifts * 2
            return jnp.concatenate(scales, axis=1), jnp.concatenate(shifts, axis=1)

        def norm(j, s, b, affine):
            rows = ROWS[s]
            m = 64 * rows
            lo = BLOCK * b
            z = jnp.maximum(acc[j, 0:m, lo:lo + BLOCK] * affine[0] + affine[1], 0.0).reshape(4, rows, 16, BLOCK)
            if s == 5:
                for h in range(4):
                    for l in range(2):
                        for t in range(2):
                            fst[j, 2 * (4 * h + b) + t, pl.ds(l, 16, stride=2), :] = z[h, l, :, LANE * t:LANE * t + LANE]
                return
            ref = (zd1, zr1, zd2, zr2, zd3)[s]
            ref[j, :, 1:1 + rows, :, lo:lo + BLOCK] = z.astype(BF)
            edge = pltpu.roll(z[:, rows - 1].reshape(64, BLOCK), 1, axis=0)
            ref[j, :, 0, :, lo:lo + BLOCK] = jnp.where(top, 0.0, edge).reshape(4, 16, BLOCK).astype(BF)
            if s in (0, 2, 4):
                edge = pltpu.roll(z[:, 0].reshape(64, BLOCK), 63, axis=0)
                ref[j, :, 1 + rows, :, lo:lo + BLOCK] = jnp.where(bottom, 0.0, edge).reshape(4, 16, BLOCK).astype(BF)

        def out_copy(n, k):
            d, dev = peer(k)
            return pltpu.make_async_remote_copy(
                src_ref=outb.at[n, d], dst_ref=o_ref.at[me * share + n], send_sem=send_out, recv_sem=recv_out,
                device_id=dev, device_id_type=MESH)

        def own_copy(n):
            return pltpu.make_async_copy(outb.at[n, me], o_ref.at[me * share + n], local_out)

        def emit(j, n):
            for d in range(16):
                outb[n, d] = jnp.concatenate([fst[j, 2 * d], fst[j, 2 * d + 1]], axis=1).astype(BF)
            own_copy(n).start()
            for k in range(1, 16):
                out_copy(n, k).start()

        def pair_body(p, carry):
            pair_head(p)
            return carry

        def pair_head(p):
            ch = p // 2

            @pl.when(lax.rem(p, 2) == 0)
            def _():
                pltpu.make_async_copy(recv.at[ch, 0:15], recv.at[ch, 0:15], recv_in.at[ch]).wait()
                wide = jnp.concatenate([
                    jnp.concatenate([recv[ch, 4 * h + w] for h in range(4)], axis=0) for w in range(4)], axis=1)
                spread = jnp.dot(wide, smat[...], preferred_element_type=F32)
                for half in range(2):
                    even = spread[:, BLOCK * half:BLOCK * half + LANE].astype(BF).reshape(4, 4, 16, LANE)
                    odd = spread[:, BLOCK * half + LANE:BLOCK * half + BLOCK].reshape(4, 4, 16, LANE)
                    ze[:, 4 * half:4 * half + 4] = even
                    zo[:, 1 + 4 * half:5 + 4 * half] = odd.astype(BF)
                    if half == 1:
                        edge = pltpu.roll(odd[:, 3].reshape(64, LANE), 1, axis=0)
                        edge = jnp.where(iota((64, LANE), 0) == 0, 0.0, edge)
                        zo[:, 0] = edge.astype(BF).reshape(4, 16, LANE)

            base = 2 * lax.rem(p, 2)
            waiting = None
            for s in range(6):
                for j in range(2):
                    parts = []
                    for b in range(4):
                        parts.append(conv(j, s, b, base + j))
                        if waiting is not None:
                            norm(*waiting[0:2], b, waiting[2])
                    waiting = (j, s, finish(s, parts))
                    if s == 5 and j == 1:
                        emit(0, 2 * p)
            for b in range(4):
                norm(*waiting[0:2], b, waiting[2])
            emit(1, 2 * p + 1)

        lax.fori_loop(0, share // 2, pair_body, 0)

        pltpu.make_async_copy(slab.at[:, 0:15], slab.at[:, 0:15], send_in).wait()
        pltpu.make_async_copy(outb.at[:, 0:15], outb.at[:, 0:15], send_out).wait()
        pltpu.make_async_copy(o_ref.at[0:15 * share], o_ref.at[0:15 * share], recv_out).wait()
        pltpu.make_async_copy(o_ref.at[0:share], o_ref.at[0:share], local_out).wait()

    return kernel


def encode(tile, params):
    count = tile.shape[0]
    share = count // 16
    chunks = share // 4
    rows = tile.reshape(count, BLOCK, 8).transpose(0, 2, 1).reshape(count * 8, BLOCK)
    weights = []
    for n, param in enumerate(params):
        if n == 0:
            weights.append(param.reshape(3, 3, 64))
        elif n % 2 == 0:
            weights.append(param.reshape(3, 3 * param.shape[2], param.shape[3]))
        else:
            weights.append(param)
    vmem = pl.BlockSpec(memory_space=pltpu.VMEM)
    return pl.pallas_call(
        make_kernel(share),
        out_shape=jax.ShapeDtypeStruct((count, 32, BLOCK), BF),
        in_specs=[vmem] * 13,
        out_specs=pl.BlockSpec(memory_space=pl.ANY),
        scratch_shapes=[
            pltpu.VMEM((chunks, 16, 64, LANE), BF),
            pltpu.VMEM((chunks, 16, 64, LANE), BF),
            pltpu.VMEM((4, 8, 16, LANE), BF),
            pltpu.VMEM((4, 9, 16, LANE), BF),
            pltpu.VMEM((4, 384, WIDE), BF),
            pltpu.VMEM((3, 512, BLOCK), BF),
            pltpu.VMEM((3, 384, BLOCK), BF),
            pltpu.VMEM((3, 512, BLOCK), BF),
            pltpu.VMEM((6, 8, LANE), F32),
            pltpu.VMEM((3, 384, LANE), BF),
            pltpu.VMEM((512, 512), BF),
            pltpu.VMEM((BLOCK, BLOCK), BF),
            pltpu.VMEM((2, 512, WIDE), F32),
            pltpu.VMEM((2, 4, 10, 16, WIDE), BF),
            pltpu.VMEM((2, 4, 9, 16, WIDE), BF),
            pltpu.VMEM((2, 4, 6, 16, WIDE), BF),
            pltpu.VMEM((2, 4, 5, 16, WIDE), BF),
            pltpu.VMEM((2, 4, 4, 16, WIDE), BF),
            pltpu.VMEM((2, 32, 32, LANE), F32),
            pltpu.VMEM((share, 16, 32, BLOCK), BF),
            pltpu.SemaphoreType.DMA,
            pltpu.SemaphoreType.DMA((chunks,)),
            pltpu.SemaphoreType.DMA,
            pltpu.SemaphoreType.DMA,
            pltpu.SemaphoreType.DMA,
        ],
        compiler_params=pltpu.CompilerParams(
            collective_id=0, has_side_effects=True, vmem_limit_bytes=60 * WIDE * WIDE),
        name="encoder",
    )(rows, *weights)


def solution(mesh):
    act_spec = P("batch", "h", "w")

    def local_forward(tile, *params):
        return encode(tile, params)[:, :, None, :]

    return jax.shard_map(local_forward, mesh=mesh, in_specs=(act_spec,) + (P(),) * 12, out_specs=act_spec, check_vma=False)
```

time: 343 us -> 122 us (0.36); the launches traced: 337 us -> 121 us
  matrix products: 195 us -> 0 us
  Pallas kernels: 0 us -> 118 us
  blocking collectives: 76.7 us -> 0 us
  local copies, waits for them, and re-layouts: 35.8 us -> 3.86 us
  waiting for transfers between devices: 15.4 us -> 0 us
  starting transfers between devices: 7.58 us -> 0 us
  other arithmetic: 5.61 us -> 0 us
    conv_general_dilated x6 -> x0, matrix products: 195 us -> none  [conv_norm(): lax.conv_general_dilated(inputs, kernel, (stride, stride), ((1, 1), (1, 1...]
    pallas_call x0 -> x1, Pallas kernels: none -> 118 us  [encode(): pl.pallas_call(make_kernel(share), out_shape=jax.ShapeDtypeStruct((count,...]
    all_to_all x1 -> x0, blocking collectives: 76.7 us -> none  [local_forward(): back = lax.all_to_all(back, ('h', 'w'), 0, 0, tiled=True)]
    reshape x15 -> x0, local copies, waits for them, and re-layouts: 24 us -> none  [the longest x2 21.1 us: local_forward(): got.transpose(2, 0, 3, 1, 4).reshape(share, rows * height, cols * width, 1)]
    all_to_all x1 -> x0, waiting for transfers between devices: 15.4 us -> none  [local_forward(): got = lax.all_to_all(sent, ('h', 'w'), 0, 0, tiled=True)]
    all_to_all x1 -> x0, starting transfers between devices: 7.58 us -> none  [local_forward(): got = lax.all_to_all(sent, ('h', 'w'), 0, 0, tiled=True)]
    convert_element_type x1 -> x0, other arithmetic: 4.88 us -> none  [conv_norm(): jax.nn.relu(summed * chan_scale[:, None, None, :] + chan_shift[:, None, N...]
  transfers between devices with their start and end apart: 1 -> 0, of which waited for: 1 -> 0; matrix products, arithmetic and copies ran while one was open for 2% -> 0% of each run, Pallas kernels for 0% -> 0%
where the time goes in v2:
time: 122 us; the launch traced here: 121 us
  Pallas kernels  118 us (97%)
  local copies, waits for them, and re-layouts  3.86 us (3%)
    pallas_call x1, Pallas kernels, encode(): pl.pallas_call(make_kernel(share), out_shape=jax.ShapeDtypeStruct((count,...  118 us
    unnamed x1, local copies, waits for them, and re-layouts  3.86 us

profile of v2, /device:TPU:0, one launch (start us, length us, event | category | flops | bytes accessed | tf_op | source)
XLA Modules:
  0.0 121.5 jit_solution(8768290371335717037)
XLA Ops:
  0.0 117.6 %encoder.1 = bf16[192,32,256]{2,1,0:T(8,128)(2,1)} custom-call(bf16[1536,256]{1,0:T(8,128)(2,1)} %bitcast.16, bf16[3,3,64]{2,1,0:T(4,128)(2,1)} %bitcast.21, f32[3,64]{1,0:T(4,128)} %v1d.1, bf16[3,192,64]{2,1,0:T(8,128)(2,1)} %bitcast.19, f32[3,64]{1,0:T(4,128)} %v1r.1, bf16[3,192,128]{2,1,0:T(8,128)(2,1)} %bitcast.20, f32[3,128]{1,0:T(4,128)} %v2d.1, ...), custom_call_target="tpu_custom_call" | custom-call | tf_op jit(solution)/shard_map/encoder/pallas_call | solution.py:289
  117.6 3.9 %copy.16 = bf16[192,32,1,256]{3,1,2,0:T(8,128)(2,1)} copy(bf16[192,32,1,256]{3,1,2,0:T(8,128)(2,1)} %bitcast.14) | data formatting | bytes 6291456

commit v3 on v2

--- a/solution.py
+++ b/solution.py
@@ -9,6 +9,7 @@
 LANE = 128
 BLOCK = 256
 WIDE = 1024
+CHUNK = 512
 BF = jnp.bfloat16
 F32 = jnp.float32
 MESH = pl.DeviceIdType.MESH
@@ -115,43 +116,50 @@
         top = iota((64, BLOCK), 0) == 0
         bottom = iota((64, BLOCK), 0) == 63
 
-        def taps(ref, j, rows, stride, lo, hi_):
+        def taps(ref, j, rows, stride, lo, hi_, h0, h1):
             pieces = []
             for dh in range(3):
                 if stride == 1:
-                    piece = ref[j, :, dh:dh + rows, :, lo:hi_]
-                    pieces.append(piece.reshape(64 * rows, hi_ - lo))
+                    piece = ref[j, h0:h1, dh:dh + rows, :, lo:hi_]
+                    pieces.append(piece.reshape((h1 - h0) * 16 * rows, hi_ - lo))
                 else:
                     pieces.append(jnp.concatenate(
-                        [ref[j, h, 2 * l + dh, :, lo:hi_] for h in range(4) for l in range(rows)], axis=0))
+                        [ref[j, h, 2 * l + dh, :, lo:hi_] for h in range(h0, h1) for l in range(rows)], axis=0))
             return jnp.concatenate(pieces, axis=1)
 
         def conv(j, s, b, i):
             rows = ROWS[s]
-            m = 64 * rows
             lo = BLOCK * b
-            if s == 0:
-                lhs = jnp.concatenate([zo[:, 0:8].reshape(m, LANE), ze[...].reshape(m, LANE),
-                                       zo[:, 1:9].reshape(m, LANE)], axis=1)
-                rhs = t1[i, :, lo:lo + BLOCK]
-            elif s in (1, 3):
-                ref, mat = ((zd1, tr1), (zd2, tr2))[s // 2]
-                first, last = (LANE if b == 0 else 0), (384 if b == 3 else 512)
-                lhs = taps(ref, j, rows, 1, lo - LANE + first, lo - LANE + last)
-                rhs = mat[:, first:last, :].reshape(3 * (last - first), BLOCK)
-            elif s in (2, 4):
-                ref, mat = ((zr1, td2), (zr2, w3d))[s // 2 - 1]
-                first = LANE if b == 0 else 0
-                lhs = taps(ref, j, rows, 2, lo - LANE + first, lo + BLOCK)
-                rhs = mat[:, first:384, :].reshape(3 * (384 - first), BLOCK)
-            else:
-                first, last = (BLOCK if b == 0 else 0), (512 if b == 3 else 768)
-                lhs = taps(zd3, j, rows, 1, lo - BLOCK + first, lo - BLOCK + last)
-                rhs = w3r[:, first:last, :].reshape(3 * (last - first), BLOCK)
-            out = jnp.dot(lhs, rhs, preferred_element_type=F32)
-            acc[j, 0:m, lo:lo + BLOCK] = out
-            tall = out.reshape(m // 8, 8, BLOCK)
-            return jnp.sum(tall, axis=0), jnp.sum(tall * tall, axis=0)
+            step = min(4, CHUNK // (16 * rows))
+            sums = sqs = None
+            for h0 in range(0, 4, step):
+                h1 = h0 + step
+                m = 16 * rows * step
+                if s == 0:
+                    lhs = jnp.concatenate([zo[h0:h1, 0:8].reshape(m, LANE), ze[h0:h1].reshape(m, LANE),
+                                           zo[h0:h1, 1:9].reshape(m, LANE)], axis=1)
+                    rhs = t1[i, :, lo:lo + BLOCK]
+                elif s in (1, 3):
+                    ref, mat = ((zd1, tr1), (zd2, tr2))[s // 2]
+                    first, last = (LANE if b == 0 else 0), (384 if b == 3 else 512)
+                    lhs = taps(ref, j, rows, 1, lo - LANE + first, lo - LANE + last, h0, h1)
+                    rhs = mat[:, first:last, :].reshape(3 * (last - first), BLOCK)
+                elif s in (2, 4):
+                    ref, mat = ((zr1, td2), (zr2, w3d))[s // 2 - 1]
+                    first = LANE if b == 0 else 0
+                    lhs = taps(ref, j, rows, 2, lo - LANE + first, lo + BLOCK, h0, h1)
+                    rhs = mat[:, first:384, :].reshape(3 * (384 - first), BLOCK)
+                else:
+                    first, last = (BLOCK if b == 0 else 0), (512 if b == 3 else 768)
+                    lhs = taps(zd3, j, rows, 1, lo - BLOCK + first, lo - BLOCK + last, h0, h1)
+                    rhs = w3r[:, first:last, :].reshape(3 * (last - first), BLOCK)
+                out = jnp.dot(lhs, rhs, preferred_element_type=F32)
+                at = 16 * rows * h0
+                acc[j, at:at + m, lo:lo + BLOCK] = out
+                tall = out.reshape(m // 8, 8, BLOCK)
+                one, two = jnp.sum(tall, axis=0), jnp.sum(tall * tall, axis=0)
+                sums, sqs = (one, two) if sums is None else (sums + one, sqs + two)
+            return sums, sqs
 
         def finish(s, parts):
             m, chan = 64 * ROWS[s], CHANS[s]
@@ -319,7 +327,7 @@
             pltpu.SemaphoreType.DMA,
         ],
         compiler_params=pltpu.CompilerParams(
-            collective_id=0, has_side_effects=True, vmem_limit_bytes=60 * WIDE * WIDE),
+            collective_id=0, has_side_effects=True, vmem_limit_bytes=30 * WIDE * WIDE),
         name="encoder",
     )(rows, *weights)
 

time: 122 us -> 113 us (0.926)
  Pallas kernels: 118 us -> 99.6 us
  local copies, waits for them, and re-layouts: 3.86 us -> 12.7 us
    pallas_call x1, Pallas kernels: 118 us -> 99.6 us  [encode(): pl.pallas_call(make_kernel(share), out_shape=jax.ShapeDtypeStruct((count,...]
    unnamed x1 -> x27, local copies, waits for them, and re-layouts: 3.86 us -> 12.7 us
where the time goes in v3:
time: 113 us; the launch traced here: 112 us
  Pallas kernels  99.6 us (88%)
  local copies, waits for them, and re-layouts  12.7 us (11%)
    pallas_call x1, Pallas kernels, encode(): pl.pallas_call(make_kernel(share), out_shape=jax.ShapeDtypeStruct((count,...  99.6 us
    unnamed x27, local copies, waits for them, and re-layouts  12.7 us

profile of v3, /device:TPU:0, one launch (start us, length us, event | category | flops | bytes accessed | tf_op | source)
XLA Modules:
  0.0 112.3 jit_solution(5010630158969708194)
XLA Ops:
  0.0 0.0 copy-start
  0.0 1.3 %copy-done = bf16[3,3,256,256]{3,2,1,0:T(8,128)(2,1)S(1)} copy-done((bf16[3,3,256,256]{3,2,1,0:T(8,128)(2,1)S(1)}, bf16[3,3,256,256]{3,2,1,0:T(8,128)(2,1)}, u32[]{:S(2)}) %copy-start) | copy-done | bytes 1179672
  1.3 0.0 copy-start.1
  1.3 1.1 %copy-done.1 = bf16[192,256,8,1]{1,2,3,0:T(8,128)(2,1)S(1)} copy-done((bf16[192,256,8,1]{1,2,3,0:T(8,128)(2,1)S(1)}, bf16[192,256,8,1]{1,2,3,0:T(8,128)(2,1)}, u32[]{:S(2)}) %copy-start.1) | copy-done | bytes 786456
  2.4 0.0 copy-start.2
  2.4 1.1 copy-done.2
  3.5 0.0 copy-start.3
  3.5 1.0 copy-done.3
  4.4 0.0 copy-start.4
  4.4 0.9 copy-done.4
  5.3 0.0 copy-start.5
  5.3 0.9 copy-done.5
  6.3 0.0 copy-start.6
  6.3 0.7 copy-done.6
  6.9 0.0 copy-start.7
  6.9 0.7 copy-done.7
  7.6 0.0 copy-start.8
  7.6 0.7 copy-done.8
  8.3 0.0 copy-start.9
  8.3 0.7 copy-done.9
  9.0 0.0 copy-start.10
  9.0 0.7 copy-done.10
  9.7 0.0 copy-start.11
  9.7 0.7 copy-done.11
  10.4 0.0 copy-start.12
  10.4 0.7 copy-done.12
  11.0 99.6 %encoder.1 = bf16[192,32,256]{2,1,0:T(8,128)(2,1)S(1)} custom-call(bf16[1536,256]{1,0:T(8,128)(2,1)S(1)} %bitcast.16, bf16[3,3,64]{2,1,0:T(4,128)(2,1)S(1)} %bitcast.21, f32[3,64]{1,0:T(4,128)S(1)} %copy-done.9, bf16[3,192,64]{2,1,0:T(8,128)(2,1)S(1)} %bitcast.19, f32[3,64]{1,0:T(4,128)S(1)} %copy-done.10, bf16[3,192,128]{2,1,0:T(8,128)(2,1)S(1)} %bitcast.20, ...), custom_call_target="tpu_custom_call" | custom-call | tf_op jit(solution)/shard_map/encoder/pallas_call | solution.py:297
  110.6 1.7 %copy.16 = bf16[192,32,1,256]{3,1,2,0:T(8,128)(2,1)} copy(bf16[192,32,1,256]{3,1,2,0:T(8,128)(2,1)S(1)} %bitcast.14) | data formatting | bytes 6291456
Async XLA Ops:
  0.0 1.3 %copy-start = (bf16[3,3,256,256]{3,2,1,0:T(8,128)(2,1)S(1)}, bf16[3,3,256,256]{3,2,1,0:T(8,128)(2,1)}, u32[]{:S(2)}) copy-start(bf16[3,3,256,256]{3,2,1,0:T(8,128)(2,1)} %param.24) | copy-start | bytes 3538948
  1.3 1.1 %copy-start.1 = (bf16[192,256,8,1]{1,2,3,0:T(8,128)(2,1)S(1)}, bf16[192,256,8,1]{1,2,3,0:T(8,128)(2,1)}, u32[]{:S(2)}) copy-start(bf16[192,256,8,1]{1,2,3,0:T(8,128)(2,1)} %param.13) | copy-start | bytes 2359300
  2.4 1.1 copy-start.2
  3.5 1.0 copy-start.3
  4.4 0.9 copy-start.4
  5.3 0.9 copy-start.5
  6.3 0.7 copy-start.6
  6.9 0.7 copy-start.7
  7.6 0.7 copy-start.8
  8.3 0.7 copy-start.9
  9.0 0.7 copy-start.10
  9.7 0.7 copy-start.11
  10.4 0.7 copy-start.12

commit v4 on v3

--- a/solution.py
+++ b/solution.py
@@ -10,6 +10,7 @@
 BLOCK = 256
 WIDE = 1024
 CHUNK = 512
+ARGS = 13
 BF = jnp.bfloat16
 F32 = jnp.float32
 MESH = pl.DeviceIdType.MESH
@@ -24,10 +25,19 @@
 def make_kernel(share):
     chunks = share // 4
 
-    def kernel(x_ref, w1d, v1d, w1r, v1r, w2d, v2d, w2r, v2r, w3d, v3d, w3r, v3r, o_ref,
+    def kernel(*refs):
+        inputs, (o_ref, *refs) = refs[:ARGS], refs[ARGS:]
+        local, refs = refs[:ARGS], refs[ARGS:]
+        body(inputs, local, o_ref, *refs)
+
+    def body(inputs, local, o_ref, load_sem,
                slab, recv, ze, zo, t1, tr1, td2, tr2, aff, gmat, smat, pmat,
                acc, zd1, zr1, zd2, zr2, zd3, fst, outb,
                send_in, recv_in, send_out, recv_out, local_out):
+        x_ref, w1d, v1d, w1r, v1r, w2d, v2d, w2r, v2r, w3d, v3d, w3r, v3r = local
+        loads = [pltpu.make_async_copy(inputs[n], local[n], load_sem.at[n]) for n in range(ARGS)]
+        for load in loads:
+            load.start()
         wi = lax.axis_index("w")
         hi = lax.axis_index("h")
         me = hi * 4 + wi
@@ -53,6 +63,7 @@
                     slab[ch, k, :, 32 * q:32 * q + 32] = turned[64 * q:64 * q + 64, 32 * ch:32 * ch + 32]
             return carry
 
+        loads[0].wait()
         lax.fori_loop(0, 16, pack, 0)
         pl.semaphore_wait(barrier, 15)
 
@@ -69,6 +80,8 @@
             lax.fori_loop(1, 16, send, 0)
             recv[ch, me] = slab[ch, 0]
 
+        for load in loads[1:]:
+            load.wait()
         r, c = iota((512, 512), 0), iota((512, 512), 1)
         smat[...] = ((r // LANE == (c // 8) % 4) & ((r // 32) % 4 == c // LANE) & ((r // 8) % 4 == (c // 32) % 4)
                      & (r % 8 == c % 8)).astype(F32).astype(BF)
@@ -215,21 +228,15 @@
                 edge = pltpu.roll(z[:, 0].reshape(64, BLOCK), 63, axis=0)
                 ref[j, :, 1 + rows, :, lo:lo + BLOCK] = jnp.where(bottom, 0.0, edge).reshape(4, 16, BLOCK).astype(BF)
 
-        def out_copy(n, k):
+        def out_copy(p, k):
             d, dev = peer(k)
             return pltpu.make_async_remote_copy(
-                src_ref=outb.at[n, d], dst_ref=o_ref.at[me * share + n], send_sem=send_out, recv_sem=recv_out,
-                device_id=dev, device_id_type=MESH)
-
-        def own_copy(n):
-            return pltpu.make_async_copy(outb.at[n, me], o_ref.at[me * share + n], local_out)
+                src_ref=outb.at[d, pl.ds(2 * p, 2)], dst_ref=o_ref.at[pl.ds(me * share + 2 * p, 2)],
+                send_sem=send_out, recv_sem=recv_out, device_id=dev, device_id_type=MESH)
 
         def emit(j, n):
             for d in range(16):
-                outb[n, d] = jnp.concatenate([fst[j, 2 * d], fst[j, 2 * d + 1]], axis=1).astype(BF)
-            own_copy(n).start()
-            for k in range(1, 16):
-                out_copy(n, k).start()
+                outb[d, n] = jnp.concatenate([fst[j, 2 * d], fst[j, 2 * d + 1]], axis=1).astype(BF)
 
         def pair_body(p, carry):
             pair_head(p)
@@ -265,17 +272,23 @@
                             norm(*waiting[0:2], b, waiting[2])
                     waiting = (j, s, finish(s, parts))
                     if s == 5 and j == 1:
-                        emit(0, 2 * p)
+                        @pl.when(p < share)
+                        def _():
+                            emit(0, 2 * p)
             for b in range(4):
                 norm(*waiting[0:2], b, waiting[2])
             emit(1, 2 * p + 1)
+            for k in range(1, 16):
+                out_copy(p, k).start()
 
         lax.fori_loop(0, share // 2, pair_body, 0)
 
         pltpu.make_async_copy(slab.at[:, 0:15], slab.at[:, 0:15], send_in).wait()
-        pltpu.make_async_copy(outb.at[:, 0:15], outb.at[:, 0:15], send_out).wait()
+        own = pltpu.make_async_copy(outb.at[me], o_ref.at[pl.ds(me * share, share)], local_out)
+        own.start()
+        own.wait()
+        pltpu.make_async_copy(outb.at[0:15], outb.at[0:15], send_out).wait()
         pltpu.make_async_copy(o_ref.at[0:15 * share], o_ref.at[0:15 * share], recv_out).wait()
-        pltpu.make_async_copy(o_ref.at[0:share], o_ref.at[0:share], local_out).wait()
 
     return kernel
 
@@ -293,13 +306,14 @@
             weights.append(param.reshape(3, 3 * param.shape[2], param.shape[3]))
         else:
             weights.append(param)
-    vmem = pl.BlockSpec(memory_space=pltpu.VMEM)
+    operands = [rows, *weights]
     return pl.pallas_call(
         make_kernel(share),
         out_shape=jax.ShapeDtypeStruct((count, 32, BLOCK), BF),
-        in_specs=[vmem] * 13,
+        in_specs=[pl.BlockSpec(memory_space=pltpu.HBM)] * ARGS,
         out_specs=pl.BlockSpec(memory_space=pl.ANY),
-        scratch_shapes=[
+        scratch_shapes=[pltpu.VMEM(a.shape, a.dtype) for a in operands] + [
+            pltpu.SemaphoreType.DMA((ARGS,)),
             pltpu.VMEM((chunks, 16, 64, LANE), BF),
             pltpu.VMEM((chunks, 16, 64, LANE), BF),
             pltpu.VMEM((4, 8, 16, LANE), BF),
@@ -319,7 +333,7 @@
             pltpu.VMEM((2, 4, 5, 16, WIDE), BF),
             pltpu.VMEM((2, 4, 4, 16, WIDE), BF),
             pltpu.VMEM((2, 32, 32, LANE), F32),
-            pltpu.VMEM((share, 16, 32, BLOCK), BF),
+            pltpu.VMEM((16, share, 32, BLOCK), BF),
             pltpu.SemaphoreType.DMA,
             pltpu.SemaphoreType.DMA((chunks,)),
             pltpu.SemaphoreType.DMA,
@@ -327,9 +341,9 @@
             pltpu.SemaphoreType.DMA,
         ],
         compiler_params=pltpu.CompilerParams(
-            collective_id=0, has_side_effects=True, vmem_limit_bytes=30 * WIDE * WIDE),
+            collective_id=0, has_side_effects=True, vmem_limit_bytes=57 * WIDE * WIDE),
         name="encoder",
-    )(rows, *weights)
+    )(*operands)
 
 
 def solution(mesh):

time: 113 us -> 108 us (0.956)
  the two profiles are of different devices: /device:TPU:0 before, /device:TPU:29 now
where the time goes in v4:
time: 108 us
  Pallas kernels  104 us (96%)
  local copies, waits for them, and re-layouts  3.86 us (4%)
    pallas_call x1, Pallas kernels, encode(): pl.pallas_call(make_kernel(share), out_shape=jax.ShapeDtypeStruct((count,...  104 us
    unnamed x1, local copies, waits for them, and re-layouts  3.86 us

profile of v4, /device:TPU:29, one launch (start us, length us, event | category | flops | bytes accessed | tf_op | source)
XLA Modules:
  0.0 107.8 jit_solution(363680478265933505)
XLA Ops:
  0.0 104.0 %encoder.1 = bf16[192,32,256]{2,1,0:T(8,128)(2,1)} custom-call(bf16[1536,256]{1,0:T(8,128)(2,1)} %bitcast.16, bf16[3,3,64]{2,1,0:T(4,128)(2,1)} %bitcast.21, f32[3,64]{1,0:T(4,128)} %refs_2_.1, bf16[3,192,64]{2,1,0:T(8,128)(2,1)} %bitcast.19, f32[3,64]{1,0:T(4,128)} %refs_4_.1, bf16[3,192,128]{2,1,0:T(8,128)(2,1)} %bitcast.20, f32[3,128]{1,0:T(4,128)} %refs_6_.1, ...), custom_call_target="tpu_custom_call" | custom-call | tf_op jit(solution)/shard_map/encoder/pallas_call | solution.py:310
  104.0 3.9 %copy.16 = bf16[192,32,1,256]{3,1,2,0:T(8,128)(2,1)} copy(bf16[192,32,1,256]{3,1,2,0:T(8,128)(2,1)} %bitcast.14) | data formatting | bytes 6291456

commit v5 on v4

--- a/solution.py
+++ b/solution.py
@@ -10,6 +10,8 @@
 BLOCK = 256
 WIDE = 1024
 CHUNK = 512
+PAIRS = 7
+SOLO = 5
 ARGS = 13
 BF = jnp.bfloat16
 F32 = jnp.float32
@@ -22,16 +24,14 @@
     return lax.broadcasted_iota(jnp.int32, shape, axis)
 
 
-def make_kernel(share):
-    chunks = share // 4
-
+def make_kernel(count):
     def kernel(*refs):
         inputs, (o_ref, *refs) = refs[:ARGS], refs[ARGS:]
         local, refs = refs[:ARGS], refs[ARGS:]
         body(inputs, local, o_ref, *refs)
 
     def body(inputs, local, o_ref, load_sem,
-               slab, recv, ze, zo, t1, tr1, td2, tr2, aff, gmat, smat, pmat,
+               slab, recv, zin, t1, tr1, td2, tr2, aff, gmat, smat, pmat, lanes,
                acc, zd1, zr1, zd2, zr2, zd3, fst, outb,
                send_in, recv_in, send_out, recv_out, local_out):
         x_ref, w1d, v1d, w1r, v1r, w2d, v2d, w2r, v2r, w3d, v3d, w3r, v3r = local
@@ -50,41 +50,57 @@
         for k in range(1, 16):
             pl.semaphore_signal(barrier, inc=1, device_id=peer(k)[1], device_id_type=MESH)
 
-        r, c = iota((BLOCK, BLOCK), 0), iota((BLOCK, BLOCK), 1)
-        half, parity, quarter, strip = r // LANE, (r // 64) % 2, (r // 16) % 4, r % 16
-        pmat[...] = (c == strip * 16 + half * 8 + quarter * 2 + parity).astype(F32).astype(BF)
-
-        def pack(k, carry):
-            d, _ = peer(k)
-            rows = x_ref[pl.ds(pl.multiple_of(d * (8 * share), 32), 8 * share), :]
-            turned = lax.dot_general(pmat[...], rows, (((1,), (1,)), ((), ())), preferred_element_type=F32).astype(BF)
-            for ch in range(chunks):
-                for q in range(4):
-                    slab[ch, k, :, 32 * q:32 * q + 32] = turned[64 * q:64 * q + 64, 32 * ch:32 * ch + 32]
-            return carry
+        side = wi // 2
+        twin = 2 * hi + lax.rem(wi, 2)
+
+        def first_image(p, h, w):
+            solo = 2 * SOLO * (4 * h + w) + 2 * p
+            shared = 2 * SOLO * 16 + 2 * (PAIRS - SOLO) * (2 * h + lax.rem(w, 2)) + 2 * (p - SOLO)
+            return jnp.where(p < SOLO, solo, shared) if not isinstance(p, int) else (solo if p < SOLO else shared)
+
+        r, c = iota((32, BLOCK), 0), iota((32, BLOCK), 1)
+        pmat[...] = ((c // 16 == r % 16) & ((c // 2) % 2 == r // 16)).astype(F32).astype(BF)
+        r, c = iota((LANE, BLOCK), 0) // 16, iota((LANE, BLOCK), 1)
+        lanes[...] = (((c // 4) % 4 == r // 2) & (c % 2 == r % 2)).astype(F32).astype(BF)
+
+        def pack(ch):
+            def step(t, carry):
+                wide = []
+                for k in (2 * t, 2 * t + 1):
+                    dev = peer(k)[1]
+                    at = pl.multiple_of(8 * first_image(ch, dev["h"], dev["w"]), 16)
+                    wide.append(jnp.concatenate([x_ref[pl.ds(at, 16), :]] * 8, axis=0) * lanes[...])
+                turned = lax.dot_general(pmat[...], jnp.concatenate(wide, axis=0), (((1,), (1,)), ((), ())),
+                                         preferred_element_type=F32).astype(BF)
+                slab[ch, 2 * t] = turned[:, :LANE]
+                slab[ch, 2 * t + 1] = turned[:, LANE:]
+                return carry
+            lax.fori_loop(0, 8, step, 0)
+
+        def send(ch):
+            def step(k, carry):
+                pltpu.make_async_remote_copy(
+                    src_ref=slab.at[ch, k], dst_ref=recv.at[ch, me], send_sem=send_in, recv_sem=recv_in.at[ch],
+                    device_id=peer(k)[1], device_id_type=MESH).start()
+                return carry
+            lax.fori_loop(1, 16, step, 0)
+            recv[ch, me] = slab[ch, 0]
 
         loads[0].wait()
-        lax.fori_loop(0, 16, pack, 0)
+        pack(0)
         pl.semaphore_wait(barrier, 15)
-
-        def in_copy(ch, k):
-            _, dev = peer(k)
-            return pltpu.make_async_remote_copy(
-                src_ref=slab.at[ch, k], dst_ref=recv.at[ch, me], send_sem=send_in, recv_sem=recv_in.at[ch],
-                device_id=dev, device_id_type=MESH)
-
-        for ch in range(chunks):
-            def send(k, carry, ch=ch):
-                in_copy(ch, k).start()
-                return carry
-            lax.fori_loop(1, 16, send, 0)
-            recv[ch, me] = slab[ch, 0]
+        send(0)
+        for ch in range(1, 3):
+            pack(ch)
+            send(ch)
 
         for load in loads[1:]:
             load.wait()
-        r, c = iota((512, 512), 0), iota((512, 512), 1)
-        smat[...] = ((r // LANE == (c // 8) % 4) & ((r // 32) % 4 == c // LANE) & ((r // 8) % 4 == (c // 32) % 4)
-                     & (r % 8 == c % 8)).astype(F32).astype(BF)
+        r, c = iota((512, WIDE), 0), iota((512, WIDE), 1)
+        column = (r // LANE == (c // 8) % 4) & (r % 8 == c % 8) & ((r // 32) % 4 == c // BLOCK)
+        here = (c % BLOCK < LANE) & ((c // 64) % 2 == (r // 8) % 2) & ((c // 32) % 2 == (r // 16) % 2)
+        above = (c % BLOCK >= LANE) & (c % LANE < 64) & ((c // 32) % 2 == (r // 8) % 2) & ((r // 16) % 2 == 1)
+        smat[...] = (column & (here | above)).astype(F32).astype(BF)
         r, c = iota((384, LANE), 0) % LANE, iota((384, LANE), 1)
         for s, chan in enumerate((64, LANE, BLOCK)):
             size = chan // 8
@@ -106,8 +122,9 @@
                 tap = jnp.concatenate([tap, tap], axis=1)
                 tap = jnp.concatenate([tap] * 8, axis=1)
                 base = jnp.where(row == 2 * col + dw - 1, jnp.broadcast_to(tap, (32, WIDE)), base)
-            for i in range(4):
-                t1[i, dh * LANE + 32 * i:dh * LANE + 32 * i + 32, :] = base.astype(BF)
+            for i in range(2):
+                at = LANE + 32 * i if dh == 0 else 64 * i + 32 * (dh - 1)
+                t1[i, at:at + 32, :] = base.astype(BF)
         tr1[...] = jnp.zeros_like(tr1)
         td2[...] = jnp.zeros_like(td2)
         tr2[...] = jnp.zeros_like(tr2)
@@ -125,6 +142,9 @@
                 for jo in range(2):
                     ji = jo + dw
                     tr2[dh, LANE * ji:LANE * ji + LANE, LANE * jo:LANE * jo + LANE] = tap
+        for ch in range(3, PAIRS):
+            pack(ch)
+            send(ch)
 
         top = iota((64, BLOCK), 0) == 0
         bottom = iota((64, BLOCK), 0) == 63
@@ -149,8 +169,7 @@
                 h1 = h0 + step
                 m = 16 * rows * step
                 if s == 0:
-                    lhs = jnp.concatenate([zo[h0:h1, 0:8].reshape(m, LANE), ze[h0:h1].reshape(m, LANE),
-                                           zo[h0:h1, 1:9].reshape(m, LANE)], axis=1)
+                    lhs = zin[h0:h1, 0:8].reshape(m, BLOCK)
                     rhs = t1[i, :, lo:lo + BLOCK]
                 elif s in (1, 3):
                     ref, mat = ((zd1, tr1), (zd2, tr2))[s // 2]
@@ -228,75 +247,76 @@
                 edge = pltpu.roll(z[:, 0].reshape(64, BLOCK), 63, axis=0)
                 ref[j, :, 1 + rows, :, lo:lo + BLOCK] = jnp.where(bottom, 0.0, edge).reshape(4, 16, BLOCK).astype(BF)
 
-        def out_copy(p, k):
-            d, dev = peer(k)
+        def out_copy(p, d):
+            h, w = d // 4, lax.rem(d, 4)
             return pltpu.make_async_remote_copy(
-                src_ref=outb.at[d, pl.ds(2 * p, 2)], dst_ref=o_ref.at[pl.ds(me * share + 2 * p, 2)],
-                send_sem=send_out, recv_sem=recv_out, device_id=dev, device_id_type=MESH)
+                src_ref=outb.at[d, pl.ds(2 * p, 2)], dst_ref=o_ref.at[pl.ds(first_image(p, hi, wi), 2)],
+                send_sem=send_out, recv_sem=recv_out, device_id={"h": h, "w": w}, device_id_type=MESH)
 
         def emit(j, n):
             for d in range(16):
                 outb[d, n] = jnp.concatenate([fst[j, 2 * d], fst[j, 2 * d + 1]], axis=1).astype(BF)
 
-        def pair_body(p, carry):
-            pair_head(p)
-            return carry
-
-        def pair_head(p):
-            ch = p // 2
-
-            @pl.when(lax.rem(p, 2) == 0)
-            def _():
-                pltpu.make_async_copy(recv.at[ch, 0:15], recv.at[ch, 0:15], recv_in.at[ch]).wait()
-                wide = jnp.concatenate([
-                    jnp.concatenate([recv[ch, 4 * h + w] for h in range(4)], axis=0) for w in range(4)], axis=1)
-                spread = jnp.dot(wide, smat[...], preferred_element_type=F32)
-                for half in range(2):
-                    even = spread[:, BLOCK * half:BLOCK * half + LANE].astype(BF).reshape(4, 4, 16, LANE)
-                    odd = spread[:, BLOCK * half + LANE:BLOCK * half + BLOCK].reshape(4, 4, 16, LANE)
-                    ze[:, 4 * half:4 * half + 4] = even
-                    zo[:, 1 + 4 * half:5 + 4 * half] = odd.astype(BF)
-                    if half == 1:
-                        edge = pltpu.roll(odd[:, 3].reshape(64, LANE), 1, axis=0)
-                        edge = jnp.where(iota((64, LANE), 0) == 0, 0.0, edge)
-                        zo[:, 0] = edge.astype(BF).reshape(4, 16, LANE)
-
-            base = 2 * lax.rem(p, 2)
+        def pair(p, carry):
+            pltpu.make_async_copy(recv.at[p, 0:15], recv.at[p, 0:15], recv_in.at[p]).wait()
+            wide = jnp.concatenate([
+                jnp.concatenate([recv[p, 4 * h + w] for h in range(4)], axis=0) for w in range(4)], axis=1)
+            spread = jnp.dot(wide, smat[...], preferred_element_type=F32)
+            for lq in range(4):
+                here, above = (spread[:, LANE * t:LANE * t + LANE].reshape(4, 2, 16, LANE) for t in (2 * lq, 2 * lq + 1))
+                zin[:, 2 * lq:2 * lq + 2, :, :LANE] = here.astype(BF)
+                zin[:, 2 * lq + 1:2 * lq + 3, :, LANE:] = above.astype(BF)
+            edge = pltpu.roll(above[:, 1].reshape(64, LANE), 1, axis=0)
+            edge = jnp.where(iota((64, LANE), 0) == 0, 0.0, edge)
+            zin[:, 0, :, LANE:] = edge.astype(BF).reshape(4, 16, LANE)
+
             waiting = None
             for s in range(6):
                 for j in range(2):
                     parts = []
                     for b in range(4):
-                        parts.append(conv(j, s, b, base + j))
+                        parts.append(conv(j, s, b, j))
                         if waiting is not None:
                             norm(*waiting[0:2], b, waiting[2])
                     waiting = (j, s, finish(s, parts))
-                    if s == 5 and j == 1:
-                        @pl.when(p < share)
-                        def _():
-                            emit(0, 2 * p)
+
+            @pl.when(p < PAIRS)
+            def _():
+                emit(0, 2 * p)
+
             for b in range(4):
                 norm(*waiting[0:2], b, waiting[2])
             emit(1, 2 * p + 1)
-            for k in range(1, 16):
-                out_copy(p, k).start()
-
-        lax.fori_loop(0, share // 2, pair_body, 0)
-
+
+            @pl.when(p < SOLO)
+            def _():
+                for k in range(1, 16):
+                    out_copy(p, peer(k)[0]).start()
+
+            @pl.when(p >= SOLO)
+            def _():
+                for k in range(1, 8):
+                    t = lax.rem(twin + k, 8)
+                    out_copy(p, 4 * (t // 2) + 2 * side + lax.rem(t, 2)).start()
+
+            return carry
+
+        lax.fori_loop(0, PAIRS, pair, 0)
+
+        for at, size, base in ((0, 2 * SOLO, first_image(0, hi, wi)), (2 * SOLO, 2 * (PAIRS - SOLO), first_image(SOLO, hi, wi))):
+            own = pltpu.make_async_copy(outb.at[me, at:at + size], o_ref.at[pl.ds(base, size)], local_out)
+            own.start()
+            own.wait()
         pltpu.make_async_copy(slab.at[:, 0:15], slab.at[:, 0:15], send_in).wait()
-        own = pltpu.make_async_copy(outb.at[me], o_ref.at[pl.ds(me * share, share)], local_out)
-        own.start()
-        own.wait()
-        pltpu.make_async_copy(outb.at[0:15], outb.at[0:15], send_out).wait()
-        pltpu.make_async_copy(o_ref.at[0:15 * share], o_ref.at[0:15 * share], recv_out).wait()
+        moved = o_ref.at[0:count - 2 * PAIRS]
+        pltpu.make_async_copy(moved, moved, send_out).wait()
+        pltpu.make_async_copy(moved, moved, recv_out).wait()
 
     return kernel
 
 
 def encode(tile, params):
     count = tile.shape[0]
-    share = count // 16
-    chunks = share // 4
     rows = tile.reshape(count, BLOCK, 8).transpose(0, 2, 1).reshape(count * 8, BLOCK)
     weights = []
     for n, param in enumerate(params):
@@ -308,24 +328,24 @@
             weights.append(param)
     operands = [rows, *weights]
     return pl.pallas_call(
-        make_kernel(share),
+        make_kernel(count),
         out_shape=jax.ShapeDtypeStruct((count, 32, BLOCK), BF),
         in_specs=[pl.BlockSpec(memory_space=pltpu.HBM)] * ARGS,
         out_specs=pl.BlockSpec(memory_space=pl.ANY),
         scratch_shapes=[pltpu.VMEM(a.shape, a.dtype) for a in operands] + [
             pltpu.SemaphoreType.DMA((ARGS,)),
-            pltpu.VMEM((chunks, 16, 64, LANE), BF),
-            pltpu.VMEM((chunks, 16, 64, LANE), BF),
-            pltpu.VMEM((4, 8, 16, LANE), BF),
-            pltpu.VMEM((4, 9, 16, LANE), BF),
-            pltpu.VMEM((4, 384, WIDE), BF),
+            pltpu.VMEM((PAIRS, 16, 32, LANE), BF),
+            pltpu.VMEM((PAIRS, 16, 32, LANE), BF),
+            pltpu.VMEM((4, 9, 16, BLOCK), BF),
+            pltpu.VMEM((2, BLOCK, WIDE), BF),
             pltpu.VMEM((3, 512, BLOCK), BF),
             pltpu.VMEM((3, 384, BLOCK), BF),
             pltpu.VMEM((3, 512, BLOCK), BF),
             pltpu.VMEM((6, 8, LANE), F32),
             pltpu.VMEM((3, 384, LANE), BF),
-            pltpu.VMEM((512, 512), BF),
-            pltpu.VMEM((BLOCK, BLOCK), BF),
+            pltpu.VMEM((512, WIDE), BF),
+            pltpu.VMEM((32, BLOCK), BF),
+            pltpu.VMEM((LANE, BLOCK), BF),
             pltpu.VMEM((2, 512, WIDE), F32),
             pltpu.VMEM((2, 4, 10, 16, WIDE), BF),
             pltpu.VMEM((2, 4, 9, 16, WIDE), BF),
@@ -333,9 +353,9 @@
             pltpu.VMEM((2, 4, 5, 16, WIDE), BF),
             pltpu.VMEM((2, 4, 4, 16, WIDE), BF),
             pltpu.VMEM((2, 32, 32, LANE), F32),
-            pltpu.VMEM((16, share, 32, BLOCK), BF),
+            pltpu.VMEM((16, 2 * PAIRS, 32, BLOCK), BF),
             pltpu.SemaphoreType.DMA,
-            pltpu.SemaphoreType.DMA((chunks,)),
+            pltpu.SemaphoreType.DMA((PAIRS,)),
             pltpu.SemaphoreType.DMA,
             pltpu.SemaphoreType.DMA,
             pltpu.SemaphoreType.DMA,

time: 108 us -> 104 us (0.963)
  the two profiles are of different devices: /device:TPU:29 before, /device:TPU:0 now
where the time goes in v5:
time: 104 us
  Pallas kernels  100 us (96%)
  local copies, waits for them, and re-layouts  3.86 us (4%)
    pallas_call x1, Pallas kernels, encode(): pl.pallas_call(make_kernel(count), out_shape=jax.ShapeDtypeStruct((count,...  100 us
    unnamed x1, local copies, waits for them, and re-layouts  3.86 us

profile of v5, /device:TPU:0, one launch (start us, length us, event | category | flops | bytes accessed | tf_op | source)
XLA Modules:
  0.0 103.9 jit_solution(13058290819127982188)
XLA Ops:
  0.0 100.0 %encoder.1 = bf16[192,32,256]{2,1,0:T(8,128)(2,1)} custom-call(bf16[1536,256]{1,0:T(8,128)(2,1)} %bitcast.16, bf16[3,3,64]{2,1,0:T(4,128)(2,1)} %bitcast.21, f32[3,64]{1,0:T(4,128)} %refs_2_.1, bf16[3,192,64]{2,1,0:T(8,128)(2,1)} %bitcast.19, f32[3,64]{1,0:T(4,128)} %refs_4_.1, bf16[3,192,128]{2,1,0:T(8,128)(2,1)} %bitcast.20, f32[3,128]{1,0:T(4,128)} %refs_6_.1, ...), custom_call_target="tpu_custom_call" | custom-call | tf_op jit(solution)/shard_map/encoder/pallas_call | solution.py:330
  100.0 3.9 %copy.16 = bf16[192,32,1,256]{3,1,2,0:T(8,128)(2,1)} copy(bf16[192,32,1,256]{3,1,2,0:T(8,128)(2,1)} %bitcast.14) | data formatting | bytes 6291456

commit v6 on v5

--- a/solution.py
+++ b/solution.py
@@ -6,6 +6,7 @@
 from jax.sharding import PartitionSpec as P
 
 NORM_EPS = 1e-5
+HALF = 64
 LANE = 128
 BLOCK = 256
 WIDE = 1024
@@ -98,23 +99,23 @@
             load.wait()
         r, c = iota((512, WIDE), 0), iota((512, WIDE), 1)
         column = (r // LANE == (c // 8) % 4) & (r % 8 == c % 8) & ((r // 32) % 4 == c // BLOCK)
-        here = (c % BLOCK < LANE) & ((c // 64) % 2 == (r // 8) % 2) & ((c // 32) % 2 == (r // 16) % 2)
-        above = (c % BLOCK >= LANE) & (c % LANE < 64) & ((c // 32) % 2 == (r // 8) % 2) & ((r // 16) % 2 == 1)
+        here = (c % BLOCK < LANE) & ((c // HALF) % 2 == (r // 8) % 2) & ((c // 32) % 2 == (r // 16) % 2)
+        above = (c % BLOCK >= LANE) & (c % LANE < HALF) & ((c // 32) % 2 == (r // 8) % 2) & ((r // 16) % 2 == 1)
         smat[...] = (column & (here | above)).astype(F32).astype(BF)
         r, c = iota((384, LANE), 0) % LANE, iota((384, LANE), 1)
-        for s, chan in enumerate((64, LANE, BLOCK)):
+        for s, chan in enumerate((HALF, LANE, BLOCK)):
             size = chan // 8
             gmat[s] = ((r % chan) // size == (c % chan) // size).astype(F32).astype(BF)
         for s, v in enumerate((v1d, v1r, v2d, v2r, v3d, v3r)):
             chan = CHANS[s]
-            if chan == 64:
+            if chan == HALF:
                 aff[s, 0:3, :] = jnp.concatenate([v[...], v[...]], axis=1)
             else:
                 aff[s, 0:3, :] = v[:, 0:LANE]
                 if chan == BLOCK:
                     aff[s, 3:6, :] = v[:, LANE:BLOCK]
         t1[...] = jnp.zeros_like(t1)
-        row, col = iota((32, WIDE), 0), iota((32, WIDE), 1) // 64
+        row, col = iota((32, WIDE), 0), iota((32, WIDE), 1) // HALF
         for dh in range(3):
             base = jnp.zeros((32, WIDE), F32)
             for dw in range(3):
@@ -123,21 +124,23 @@
                 tap = jnp.concatenate([tap] * 8, axis=1)
                 base = jnp.where(row == 2 * col + dw - 1, jnp.broadcast_to(tap, (32, WIDE)), base)
             for i in range(2):
-                at = LANE + 32 * i if dh == 0 else 64 * i + 32 * (dh - 1)
+                at = LANE + 32 * i if dh == 0 else HALF * i + 32 * (dh - 1)
                 t1[i, at:at + 32, :] = base.astype(BF)
         tr1[...] = jnp.zeros_like(tr1)
         td2[...] = jnp.zeros_like(td2)
         tr2[...] = jnp.zeros_like(tr2)
         for dh in range(3):
             for dw in range(3):
-                tap = w1r[dh, 64 * dw:64 * dw + 64, :]
-                for jo in range(4):
-                    ji = jo + 1 + dw
-                    tr1[dh, 64 * ji:64 * ji + 64, 64 * jo:64 * jo + 64] = tap
-                tap = w2d[dh, 64 * dw:64 * dw + 64, :]
+                tap = w1r[dh, HALF * dw:HALF * dw + HALF, :]
+                for t in range(2):
+                    for jo in range(2):
+                        row = BLOCK * (dh + t) + HALF * ((jo + dw + 3) % 4)
+                        col = LANE * t + HALF * jo
+                        tr1[row:row + HALF, col:col + HALF] = tap
+                tap = w2d[dh, HALF * dw:HALF * dw + HALF, :]
                 for jo in range(2):
                     ji = 2 * jo + 1 + dw
-                    td2[dh, 64 * ji:64 * ji + 64, LANE * jo:LANE * jo + LANE] = tap
+                    td2[dh, HALF * ji:HALF * ji + HALF, LANE * jo:LANE * jo + LANE] = tap
                 tap = w2r[dh, LANE * dw:LANE * dw + LANE, :]
                 for jo in range(2):
                     ji = jo + dw
@@ -146,8 +149,8 @@
             pack(ch)
             send(ch)
 
-        top = iota((64, BLOCK), 0) == 0
-        bottom = iota((64, BLOCK), 0) == 63
+        top = iota((HALF, BLOCK), 0) == 0
+        bottom = iota((HALF, BLOCK), 0) == 63
 
         def taps(ref, j, rows, stride, lo, hi_, h0, h1):
             pieces = []
@@ -160,9 +163,29 @@
                         [ref[j, h, 2 * l + dh, :, lo:hi_] for h in range(h0, h1) for l in range(rows)], axis=0))
             return jnp.concatenate(pieces, axis=1)
 
+        def conv_square(j, b):
+            sums = sqs = 0.0
+            for p in (2 * b, 2 * b + 1):
+                pieces = []
+                for t in range(4):
+                    for lo in (LANE * p, WIDE + LANE * p):
+                        pieces.append(jnp.concatenate(
+                            [zd1[j, h, 2 * l + t, :, lo:lo + LANE] for h in range(4) for l in range(4)], axis=0))
+                out = jnp.dot(jnp.concatenate(pieces, axis=1), tr1[...], preferred_element_type=F32)
+                tall = out.reshape(BLOCK // 8, 8, BLOCK)
+                sums, sqs = sums + jnp.sum(tall, axis=0), sqs + jnp.sum(tall * tall, axis=0)
+                out = out.reshape(16, 16, BLOCK)
+                for n in range(16):
+                    for t in range(2):
+                        at = 16 * (2 * n + t)
+                        acc[j, at:at + 16, LANE * p:LANE * p + LANE] = out[n, :, LANE * t:LANE * t + LANE]
+            return sums, sqs
+
         def conv(j, s, b, i):
             rows = ROWS[s]
             lo = BLOCK * b
+            if s == 1:
+                return conv_square(j, b)
             step = min(4, CHUNK // (16 * rows))
             sums = sqs = None
             for h0 in range(0, 4, step):
@@ -171,8 +194,8 @@
                 if s == 0:
                     lhs = zin[h0:h1, 0:8].reshape(m, BLOCK)
                     rhs = t1[i, :, lo:lo + BLOCK]
-                elif s in (1, 3):
-                    ref, mat = ((zd1, tr1), (zd2, tr2))[s // 2]
+                elif s == 3:
+                    ref, mat = zd2, tr2
                     first, last = (LANE if b == 0 else 0), (384 if b == 3 else 512)
                     lhs = taps(ref, j, rows, 1, lo - LANE + first, lo - LANE + last, h0, h1)
                     rhs = mat[:, first:last, :].reshape(3 * (last - first), BLOCK)
@@ -194,7 +217,7 @@
             return sums, sqs
 
         def finish(s, parts):
-            m, chan = 64 * ROWS[s], CHANS[s]
+            m, chan = HALF * ROWS[s], CHANS[s]
             sums = parts[0][0] + parts[1][0] + parts[2][0] + parts[3][0]
             sqs = parts[0][1] + parts[1][1] + parts[2][1] + parts[3][1]
             if chan == BLOCK:
@@ -230,7 +253,7 @@
 
         def norm(j, s, b, affine):
             rows = ROWS[s]
-            m = 64 * rows
+            m = HALF * rows
             lo = BLOCK * b
             z = jnp.maximum(acc[j, 0:m, lo:lo + BLOCK] * affine[0] + affine[1], 0.0).reshape(4, rows, 16, BLOCK)
             if s == 5:
@@ -241,11 +264,17 @@
                 return
             ref = (zd1, zr1, zd2, zr2, zd3)[s]
             ref[j, :, 1:1 + rows, :, lo:lo + BLOCK] = z.astype(BF)
-            edge = pltpu.roll(z[:, rows - 1].reshape(64, BLOCK), 1, axis=0)
+            edge = pltpu.roll(z[:, rows - 1].reshape(HALF, BLOCK), 1, axis=0)
             ref[j, :, 0, :, lo:lo + BLOCK] = jnp.where(top, 0.0, edge).reshape(4, 16, BLOCK).astype(BF)
-            if s in (0, 2, 4):
-                edge = pltpu.roll(z[:, 0].reshape(64, BLOCK), 63, axis=0)
+            if s % 2 == 0:
+                edge = pltpu.roll(z[:, 0].reshape(HALF, BLOCK), 63, axis=0)
                 ref[j, :, 1 + rows, :, lo:lo + BLOCK] = jnp.where(bottom, 0.0, edge).reshape(4, 16, BLOCK).astype(BF)
+            if s == 0:
+                for p in range(max(2 * b - 1, 0), 2 * b + 1 + b // 3):
+                    left = zd1[j, :, :, :, LANE * p - LANE:LANE * p] if p > 0 else jnp.zeros((4, 10, 16, LANE), BF)
+                    right = zd1[j, :, :, :, LANE * p + LANE:LANE * p + BLOCK] if p < 7 else jnp.zeros((4, 10, 16, LANE), BF)
+                    zd1[j, :, :, :, WIDE + LANE * p:WIDE + LANE * p + LANE] = jnp.where(
+                        iota((4, 10, 16, LANE), 3) < HALF, right, left)
 
         def out_copy(p, d):
             h, w = d // 4, lax.rem(d, 4)
@@ -266,8 +295,8 @@
                 here, above = (spread[:, LANE * t:LANE * t + LANE].reshape(4, 2, 16, LANE) for t in (2 * lq, 2 * lq + 1))
                 zin[:, 2 * lq:2 * lq + 2, :, :LANE] = here.astype(BF)
                 zin[:, 2 * lq + 1:2 * lq + 3, :, LANE:] = above.astype(BF)
-            edge = pltpu.roll(above[:, 1].reshape(64, LANE), 1, axis=0)
-            edge = jnp.where(iota((64, LANE), 0) == 0, 0.0, edge)
+            edge = pltpu.roll(above[:, 1].reshape(HALF, LANE), 1, axis=0)
+            edge = jnp.where(iota((HALF, LANE), 0) == 0, 0.0, edge)
             zin[:, 0, :, LANE:] = edge.astype(BF).reshape(4, 16, LANE)
 
             waiting = None
@@ -279,6 +308,10 @@
                         if waiting is not None:
                             norm(*waiting[0:2], b, waiting[2])
                     waiting = (j, s, finish(s, parts))
+                    if (s, j) in ((0, 0), (0, 1)):
+                        @pl.when(p < PAIRS)
+                        def _():
+                            aff[0, 7:8, :] = aff[0, 0:1, :]
 
             @pl.when(p < PAIRS)
             def _():
@@ -321,7 +354,7 @@
     weights = []
     for n, param in enumerate(params):
         if n == 0:
-            weights.append(param.reshape(3, 3, 64))
+            weights.append(param.reshape(3, 3, HALF))
         elif n % 2 == 0:
             weights.append(param.reshape(3, 3 * param.shape[2], param.shape[3]))
         else:
@@ -338,7 +371,7 @@
             pltpu.VMEM((PAIRS, 16, 32, LANE), BF),
             pltpu.VMEM((4, 9, 16, BLOCK), BF),
             pltpu.VMEM((2, BLOCK, WIDE), BF),
-            pltpu.VMEM((3, 512, BLOCK), BF),
+            pltpu.VMEM((WIDE, BLOCK), BF),
             pltpu.VMEM((3, 384, BLOCK), BF),
             pltpu.VMEM((3, 512, BLOCK), BF),
             pltpu.VMEM((6, 8, LANE), F32),
@@ -347,7 +380,7 @@
             pltpu.VMEM((32, BLOCK), BF),
             pltpu.VMEM((LANE, BLOCK), BF),
             pltpu.VMEM((2, 512, WIDE), F32),
-            pltpu.VMEM((2, 4, 10, 16, WIDE), BF),
+            pltpu.VMEM((2, 4, 10, 16, 2 * WIDE), BF),
             pltpu.VMEM((2, 4, 9, 16, WIDE), BF),
             pltpu.VMEM((2, 4, 6, 16, WIDE), BF),
             pltpu.VMEM((2, 4, 5, 16, WIDE), BF),
@@ -361,7 +394,7 @@
             pltpu.SemaphoreType.DMA,
         ],
         compiler_params=pltpu.CompilerParams(
-            collective_id=0, has_side_effects=True, vmem_limit_bytes=57 * WIDE * WIDE),
+            collective_id=0, has_side_effects=True, vmem_limit_bytes=58 * WIDE * WIDE),
         name="encoder",
     )(*operands)
 

time: 104 us -> 106 us (1.019)
  Pallas kernels: 100 us -> 102 us
    pallas_call x1, Pallas kernels: 100 us -> 102 us  [encode(): pl.pallas_call(make_kernel(count), out_shape=jax.ShapeDtypeStruct((count,...]
where the time goes in v6:
time: 106 us
  Pallas kernels  102 us (96%)
  local copies, waits for them, and re-layouts  3.86 us (4%)
    pallas_call x1, Pallas kernels, encode(): pl.pallas_call(make_kernel(count), out_shape=jax.ShapeDtypeStruct((count,...  102 us
    unnamed x1, local copies, waits for them, and re-layouts  3.86 us

profile of v6, /device:TPU:0, one launch (start us, length us, event | category | flops | bytes accessed | tf_op | source)
XLA Modules:
  0.0 106.2 jit_solution(1565924198864950534)
XLA Ops:
  0.0 102.4 %encoder.1 = bf16[192,32,256]{2,1,0:T(8,128)(2,1)} custom-call(bf16[1536,256]{1,0:T(8,128)(2,1)} %bitcast.16, bf16[3,3,64]{2,1,0:T(4,128)(2,1)} %bitcast.21, f32[3,64]{1,0:T(4,128)} %refs_2_.1, bf16[3,192,64]{2,1,0:T(8,128)(2,1)} %bitcast.19, f32[3,64]{1,0:T(4,128)} %refs_4_.1, bf16[3,192,128]{2,1,0:T(8,128)(2,1)} %bitcast.20, f32[3,128]{1,0:T(4,128)} %refs_6_.1, ...), custom_call_target="tpu_custom_call" | custom-call | tf_op jit(solution)/shard_map/encoder/pallas_call | solution.py:363
  102.4 3.9 %copy.16 = bf16[192,32,1,256]{3,1,2,0:T(8,128)(2,1)} copy(bf16[192,32,1,256]{3,1,2,0:T(8,128)(2,1)} %bitcast.14) | data formatting | bytes 6291456

commit v7 on v5

--- a/solution.py
+++ b/solution.py
@@ -12,6 +12,7 @@
 CHUNK = 512
 PAIRS = 7
 SOLO = 5
+GROUPS = ((0, 1), (1, 2), (3, 4))
 ARGS = 13
 BF = jnp.bfloat16
 F32 = jnp.float32
@@ -72,27 +73,29 @@
                     wide.append(jnp.concatenate([x_ref[pl.ds(at, 16), :]] * 8, axis=0) * lanes[...])
                 turned = lax.dot_general(pmat[...], jnp.concatenate(wide, axis=0), (((1,), (1,)), ((), ())),
                                          preferred_element_type=F32).astype(BF)
-                slab[ch, 2 * t] = turned[:, :LANE]
-                slab[ch, 2 * t + 1] = turned[:, LANE:]
+                slab[2 * t, ch] = turned[:, :LANE]
+                slab[2 * t + 1, ch] = turned[:, LANE:]
                 return carry
             lax.fori_loop(0, 8, step, 0)
 
-        def send(ch):
+        def send(g):
+            at, size = GROUPS[g]
+
             def step(k, carry):
                 pltpu.make_async_remote_copy(
-                    src_ref=slab.at[ch, k], dst_ref=recv.at[ch, me], send_sem=send_in, recv_sem=recv_in.at[ch],
-                    device_id=peer(k)[1], device_id_type=MESH).start()
+                    src_ref=slab.at[k, at:at + size], dst_ref=recv.at[me, at:at + size], send_sem=send_in,
+                    recv_sem=recv_in.at[g], device_id=peer(k)[1], device_id_type=MESH).start()
                 return carry
             lax.fori_loop(1, 16, step, 0)
-            recv[ch, me] = slab[ch, 0]
+            recv[me, at:at + size] = slab[0, at:at + size]
 
         loads[0].wait()
         pack(0)
         pl.semaphore_wait(barrier, 15)
         send(0)
-        for ch in range(1, 3):
-            pack(ch)
-            send(ch)
+        pack(1)
+        pack(2)
+        send(1)
 
         for load in loads[1:]:
             load.wait()
@@ -142,9 +145,10 @@
                 for jo in range(2):
                     ji = jo + dw
                     tr2[dh, LANE * ji:LANE * ji + LANE, LANE * jo:LANE * jo + LANE] = tap
+
         for ch in range(3, PAIRS):
             pack(ch)
-            send(ch)
+        send(2)
 
         top = iota((64, BLOCK), 0) == 0
         bottom = iota((64, BLOCK), 0) == 63
@@ -258,9 +262,14 @@
                 outb[d, n] = jnp.concatenate([fst[j, 2 * d], fst[j, 2 * d + 1]], axis=1).astype(BF)
 
         def pair(p, carry):
-            pltpu.make_async_copy(recv.at[p, 0:15], recv.at[p, 0:15], recv_in.at[p]).wait()
+            for g, (at, size) in enumerate(GROUPS):
+                @pl.when(p == at)
+                def _(g=g, size=size):
+                    arrived = recv.at[0:15, 0:size]
+                    pltpu.make_async_copy(arrived, arrived, recv_in.at[g]).wait()
+
             wide = jnp.concatenate([
-                jnp.concatenate([recv[p, 4 * h + w] for h in range(4)], axis=0) for w in range(4)], axis=1)
+                jnp.concatenate([recv[4 * h + w, p] for h in range(4)], axis=0) for w in range(4)], axis=1)
             spread = jnp.dot(wide, smat[...], preferred_element_type=F32)
             for lq in range(4):
                 here, above = (spread[:, LANE * t:LANE * t + LANE].reshape(4, 2, 16, LANE) for t in (2 * lq, 2 * lq + 1))
@@ -279,6 +288,10 @@
                         if waiting is not None:
                             norm(*waiting[0:2], b, waiting[2])
                     waiting = (j, s, finish(s, parts))
+                    if s == 0 and j == 0:
+                        @pl.when(p < PAIRS)
+                        def _():
+                            aff[0, 7:8, :] = aff[0, 0:1, :]
 
             @pl.when(p < PAIRS)
             def _():
@@ -307,7 +320,7 @@
             own = pltpu.make_async_copy(outb.at[me, at:at + size], o_ref.at[pl.ds(base, size)], local_out)
             own.start()
             own.wait()
-        pltpu.make_async_copy(slab.at[:, 0:15], slab.at[:, 0:15], send_in).wait()
+        pltpu.make_async_copy(slab.at[0:15], slab.at[0:15], send_in).wait()
         moved = o_ref.at[0:count - 2 * PAIRS]
         pltpu.make_async_copy(moved, moved, send_out).wait()
         pltpu.make_async_copy(moved, moved, recv_out).wait()
@@ -334,8 +347,8 @@
         out_specs=pl.BlockSpec(memory_space=pl.ANY),
         scratch_shapes=[pltpu.VMEM(a.shape, a.dtype) for a in operands] + [
             pltpu.SemaphoreType.DMA((ARGS,)),
-            pltpu.VMEM((PAIRS, 16, 32, LANE), BF),
-            pltpu.VMEM((PAIRS, 16, 32, LANE), BF),
+            pltpu.VMEM((16, PAIRS, 32, LANE), BF),
+            pltpu.VMEM((16, PAIRS, 32, LANE), BF),
             pltpu.VMEM((4, 9, 16, BLOCK), BF),
             pltpu.VMEM((2, BLOCK, WIDE), BF),
             pltpu.VMEM((3, 512, BLOCK), BF),
@@ -355,7 +368,7 @@
             pltpu.VMEM((2, 32, 32, LANE), F32),
             pltpu.VMEM((16, 2 * PAIRS, 32, BLOCK), BF),
             pltpu.SemaphoreType.DMA,
-            pltpu.SemaphoreType.DMA((PAIRS,)),
+            pltpu.SemaphoreType.DMA((len(GROUPS),)),
             pltpu.SemaphoreType.DMA,
             pltpu.SemaphoreType.DMA,
             pltpu.SemaphoreType.DMA,

time: 104 us -> 103 us (level)
  no operation moved by 1% of the time
where the time goes in v7:
time: 103 us
  Pallas kernels  99.2 us (96%)
  local copies, waits for them, and re-layouts  3.86 us (4%)
    pallas_call x1, Pallas kernels, encode(): pl.pallas_call(make_kernel(count), out_shape=jax.ShapeDtypeStruct((count,...  99.2 us
    unnamed x1, local copies, waits for them, and re-layouts  3.86 us

profile of v7, /device:TPU:0, one launch (start us, length us, event | category | flops | bytes accessed | tf_op | source)
XLA Modules:
  0.0 103.1 jit_solution(11746877818777086468)
XLA Ops:
  0.0 99.2 %encoder.1 = bf16[192,32,256]{2,1,0:T(8,128)(2,1)} custom-call(bf16[1536,256]{1,0:T(8,128)(2,1)} %bitcast.16, bf16[3,3,64]{2,1,0:T(4,128)(2,1)} %bitcast.21, f32[3,64]{1,0:T(4,128)} %refs_2_.1, bf16[3,192,64]{2,1,0:T(8,128)(2,1)} %bitcast.19, f32[3,64]{1,0:T(4,128)} %refs_4_.1, bf16[3,192,128]{2,1,0:T(8,128)(2,1)} %bitcast.20, f32[3,128]{1,0:T(4,128)} %refs_6_.1, ...), custom_call_target="tpu_custom_call" | custom-call | tf_op jit(solution)/shard_map/encoder/pallas_call | solution.py:343
  99.2 3.9 %copy.16 = bf16[192,32,1,256]{3,1,2,0:T(8,128)(2,1)} copy(bf16[192,32,1,256]{3,1,2,0:T(8,128)(2,1)} %bitcast.14) | data formatting | bytes 6291456

commit v8 on v7

--- a/solution.py
+++ b/solution.py
@@ -286,8 +286,13 @@
                     for b in range(4):
                         parts.append(conv(j, s, b, j))
                         if waiting is not None:
-                            norm(*waiting[0:2], b, waiting[2])
-                    waiting = (j, s, finish(s, parts))
+                            if b == 0:
+                                affine = finish(waiting[1], waiting[2])
+                            else:
+                                norm(*waiting[0:2], b - 1, affine)
+                            if b == 3:
+                                norm(*waiting[0:2], b, affine)
+                    waiting = (j, s, parts)
                     if s == 0 and j == 0:
                         @pl.when(p < PAIRS)
                         def _():
@@ -297,8 +302,9 @@
             def _():
                 emit(0, 2 * p)
 
+            affine = finish(waiting[1], waiting[2])
             for b in range(4):
-                norm(*waiting[0:2], b, waiting[2])
+                norm(*waiting[0:2], b, affine)
             emit(1, 2 * p + 1)
 
             @pl.when(p < SOLO)

time: 103 us -> 99.6 us (0.967)
  Pallas kernels: 99.2 us -> 95.6 us
    pallas_call x1, Pallas kernels: 99.2 us -> 95.6 us  [encode(): pl.pallas_call(make_kernel(count), out_shape=jax.ShapeDtypeStruct((count,...]
where the time goes in v8:
time: 99.6 us; the launch traced here: 99.5 us
  Pallas kernels  95.6 us (96%)
  local copies, waits for them, and re-layouts  3.86 us (4%)
    pallas_call x1, Pallas kernels, encode(): pl.pallas_call(make_kernel(count), out_shape=jax.ShapeDtypeStruct((count,...  95.6 us
    unnamed x1, local copies, waits for them, and re-layouts  3.86 us

profile of v8, /device:TPU:0, one launch (start us, length us, event | category | flops | bytes accessed | tf_op | source)
XLA Modules:
  0.0 99.5 jit_solution(9930964453670948234)
XLA Ops:
  0.0 95.6 %encoder.1 = bf16[192,32,256]{2,1,0:T(8,128)(2,1)} custom-call(bf16[1536,256]{1,0:T(8,128)(2,1)} %bitcast.16, bf16[3,3,64]{2,1,0:T(4,128)(2,1)} %bitcast.21, f32[3,64]{1,0:T(4,128)} %refs_2_.1, bf16[3,192,64]{2,1,0:T(8,128)(2,1)} %bitcast.19, f32[3,64]{1,0:T(4,128)} %refs_4_.1, bf16[3,192,128]{2,1,0:T(8,128)(2,1)} %bitcast.20, f32[3,128]{1,0:T(4,128)} %refs_6_.1, ...), custom_call_target="tpu_custom_call" | custom-call | tf_op jit(solution)/shard_map/encoder/pallas_call | solution.py:349
  95.6 3.9 %copy.16 = bf16[192,32,1,256]{3,1,2,0:T(8,128)(2,1)} copy(bf16[192,32,1,256]{3,1,2,0:T(8,128)(2,1)} %bitcast.14) | data formatting | bytes 6291456

commit v9 on v8

--- a/solution.py
+++ b/solution.py
@@ -6,6 +6,7 @@
 from jax.sharding import PartitionSpec as P
 
 NORM_EPS = 1e-5
+SPAN = 512
 LANE = 128
 BLOCK = 256
 WIDE = 1024
@@ -14,6 +15,7 @@
 SOLO = 5
 GROUPS = ((0, 1), (1, 2), (3, 4))
 ARGS = 13
+STEPS = 8
 BF = jnp.bfloat16
 F32 = jnp.float32
 MESH = pl.DeviceIdType.MESH
@@ -99,7 +101,7 @@
 
         for load in loads[1:]:
             load.wait()
-        r, c = iota((512, WIDE), 0), iota((512, WIDE), 1)
+        r, c = iota((SPAN, WIDE), 0), iota((SPAN, WIDE), 1)
         column = (r // LANE == (c // 8) % 4) & (r % 8 == c % 8) & ((r // 32) % 4 == c // BLOCK)
         here = (c % BLOCK < LANE) & ((c // 64) % 2 == (r // 8) % 2) & ((c // 32) % 2 == (r // 16) % 2)
         above = (c % BLOCK >= LANE) & (c % LANE < 64) & ((c // 32) % 2 == (r // 8) % 2) & ((r // 16) % 2 == 1)
@@ -177,7 +179,7 @@
                     rhs = t1[i, :, lo:lo + BLOCK]
                 elif s in (1, 3):
                     ref, mat = ((zd1, tr1), (zd2, tr2))[s // 2]
-                    first, last = (LANE if b == 0 else 0), (384 if b == 3 else 512)
+                    first, last = (LANE if b == 0 else 0), (384 if b == 3 else SPAN)
                     lhs = taps(ref, j, rows, 1, lo - LANE + first, lo - LANE + last, h0, h1)
                     rhs = mat[:, first:last, :].reshape(3 * (last - first), BLOCK)
                 elif s in (2, 4):
@@ -186,7 +188,7 @@
                     lhs = taps(ref, j, rows, 2, lo - LANE + first, lo + BLOCK, h0, h1)
                     rhs = mat[:, first:384, :].reshape(3 * (384 - first), BLOCK)
                 else:
-                    first, last = (BLOCK if b == 0 else 0), (512 if b == 3 else 768)
+                    first, last = (BLOCK if b == 0 else 0), (SPAN if b == 3 else 768)
                     lhs = taps(zd3, j, rows, 1, lo - BLOCK + first, lo - BLOCK + last, h0, h1)
                     rhs = w3r[:, first:last, :].reshape(3 * (last - first), BLOCK)
                 out = jnp.dot(lhs, rhs, preferred_element_type=F32)
@@ -357,15 +359,15 @@
             pltpu.VMEM((16, PAIRS, 32, LANE), BF),
             pltpu.VMEM((4, 9, 16, BLOCK), BF),
             pltpu.VMEM((2, BLOCK, WIDE), BF),
-            pltpu.VMEM((3, 512, BLOCK), BF),
+            pltpu.VMEM((3, SPAN, BLOCK), BF),
             pltpu.VMEM((3, 384, BLOCK), BF),
-            pltpu.VMEM((3, 512, BLOCK), BF),
+            pltpu.VMEM((3, SPAN, BLOCK), BF),
             pltpu.VMEM((6, 8, LANE), F32),
             pltpu.VMEM((3, 384, LANE), BF),
-            pltpu.VMEM((512, WIDE), BF),
+            pltpu.VMEM((SPAN, WIDE), BF),
             pltpu.VMEM((32, BLOCK), BF),
             pltpu.VMEM((LANE, BLOCK), BF),
-            pltpu.VMEM((2, 512, WIDE), F32),
+            pltpu.VMEM((2, SPAN, WIDE), F32),
             pltpu.VMEM((2, 4, 10, 16, WIDE), BF),
             pltpu.VMEM((2, 4, 9, 16, WIDE), BF),
             pltpu.VMEM((2, 4, 6, 16, WIDE), BF),
@@ -385,10 +387,31 @@
     )(*operands)
 
 
+def hand_over(part):
+    size = part.shape[0] // STEPS
+
+    def kernel(src, dst, held, load_sem, store_sem):
+        loads, stores = ([pltpu.make_async_copy(a.at[size * n:size * n + size], b.at[size * n:size * n + size], c.at[n])
+                          for n in range(STEPS)] for a, b, c in ((src, held, load_sem), (held, dst, store_sem)))
+        for load in loads:
+            load.start()
+        for load, store in zip(loads, stores):
+            load.wait()
+            store.start()
+        for store in stores:
+            store.wait()
+
+    anywhere = pl.BlockSpec(memory_space=pltpu.HBM)
+    return pl.pallas_call(
+        kernel, out_shape=jax.ShapeDtypeStruct(part.shape, part.dtype), in_specs=[anywhere], out_specs=anywhere,
+        scratch_shapes=[pltpu.VMEM(part.shape, part.dtype), pltpu.SemaphoreType.DMA((STEPS,)), pltpu.SemaphoreType.DMA((STEPS,))],
+        compiler_params=pltpu.CompilerParams(vmem_limit_bytes=58 * WIDE * WIDE), name="hand_over")(part)
+
+
 def solution(mesh):
     act_spec = P("batch", "h", "w")
 
     def local_forward(tile, *params):
-        return encode(tile, params)[:, :, None, :]
+        return hand_over(encode(tile, params))[:, :, None, :]
 
     return jax.shard_map(local_forward, mesh=mesh, in_specs=(act_spec,) + (P(),) * 12, out_specs=act_spec, check_vma=False)

time: 99.6 us -> 98.6 us (0.990)
  local copies, waits for them, and re-layouts: 3.86 us -> 0 us
  Pallas kernels: 95.6 us -> 98.4 us
    unnamed x1 -> x0, local copies, waits for them, and re-layouts: 3.86 us -> none
    pallas_call x0 -> x1, Pallas kernels: none -> 2.79 us  [hand_over(): pl.pallas_call(kernel, out_shape=jax.ShapeDtypeStruct(part.shape, part.dt...]
where the time goes in v9:
time: 98.6 us; the launch traced here: 98.4 us
  Pallas kernels  98.4 us (100%)
    pallas_call x1, Pallas kernels, encode(): pl.pallas_call(make_kernel(count), out_shape=jax.ShapeDtypeStruct((count,...  95.6 us
    pallas_call x1, Pallas kernels, hand_over(): pl.pallas_call(kernel, out_shape=jax.ShapeDtypeStruct(part.shape, part.dt...  2.79 us

profile of v9, /device:TPU:0, one launch (start us, length us, event | category | flops | bytes accessed | tf_op | source)
XLA Modules:
  0.0 98.4 jit_solution(7363030015052164226)
XLA Ops:
  0.0 95.6 %encoder.1.src = bf16[192,32,256]{2,1,0:T(8,128)(2,1)} custom-call(bf16[1536,256]{1,0:T(8,128)(2,1)} %bitcast.15, bf16[3,3,64]{2,1,0:T(4,128)(2,1)} %bitcast.20, f32[3,64]{1,0:T(4,128)} %refs_2_.1, bf16[3,192,64]{2,1,0:T(8,128)(2,1)} %bitcast.18, f32[3,64]{1,0:T(4,128)} %refs_4_.1, bf16[3,192,128]{2,1,0:T(8,128)(2,1)} %bitcast.19, f32[3,128]{1,0:T(4,128)} %refs_6_.1, ...), custom_call_target="tpu_custom_call" | custom-call | tf_op jit(solution)/shard_map/encoder/pallas_call | solution.py:351
  95.6 2.8 %hand_over.1 = bf16[192,32,256]{2,1,0:T(8,128)(2,1)} custom-call(bf16[192,32,256]{2,1,0:T(8,128)(2,1)} %encoder.1.src), custom_call_target="tpu_custom_call" | custom-call | tf_op jit(solution)/shard_map/hand_over/pallas_call | solution.py:405
